TPU v7x, 256 devices: a 4x2x16 block of a 4x16x16 slice. The times are simulated.
256 devices in a mesh: grp: 2 (over y), page: 128 (over z, x, core).
Axes of the slice: x: 4, y: 2, z: 16, core: 2. Of those that a mesh axis runs over, the one named last changes fastest.
The devices are a block of a 4x16x16 slice.
Arguments:
- queries: bfloat16 [32, 4096], P('grp'), parts along dimension 0, may hold values from -64 to 64
- key_cache: bfloat16 [8192, 64, 1024], P(('grp', 'page')), parts along dimension 0, may hold values from -9 to 9
- value_cache: bfloat16 [8192, 64, 1024], P(('grp', 'page')), parts along dimension 0, may hold values from -16 to 16
- new_keys: bfloat16 [32, 1024], P('grp'), parts along dimension 0, may hold values from -16 to 16
- new_values: bfloat16 [32, 1024], P('grp'), parts along dimension 0, may hold values from -6 to 6
- chosen: int32 [16, 256], P('grp', 'page'), parts along dimension 0, may hold values from 0 to 4095, as said below
Outputs:
- attended: bfloat16 [32, 4096], P('grp'), parts along dimension 0
There are 2 independent parts, one for each index of `grp`. A program takes and returns all parts, laid end to end along the dimension named above; each array names one. Nothing has to cross between parts.
Inputs may be any that keep to these rules, and one draw needn't show every extreme that they name: `chosen`: each row names 256 different pages; at most 8 of a row's pages lie in the range of 32 pages of one device, and exactly 8 do for some device in every row.
All inputs are finite; a program needn't handle non-finite values.
Results may differ from a plain program's by a relative error of at most 0.004.
Values may be sent and summed in bfloat16 or wider, within the bound.
A program may use at most 64 MiB of HBM per device.

v0:
```python
import jax
import jax.numpy as jnp
from jax import lax
from jax.sharding import Mesh
from jax.sharding import PartitionSpec as P

PAGE = ("page_0", "page_1", "page_2")
GRP_PAGE = ("grp", "page_0", "page_1", "page_2")


FLOOR_SCORE = -1e30


def in_order(tiles, dim):
    shape = list(tiles.shape[1:])
    shape[dim] *= tiles.shape[0]
    return jnp.moveaxis(tiles, 0, dim).reshape(shape)


def gather_in_order(value, axes, sequence):
    tiles = value
    for k in sequence:
        tiles = lax.all_gather(tiles, axes[k])
    done = sequence[::-1]
    back = [done.index(k) for k in range(len(axes))]
    tiles = tiles.transpose(*back, *range(len(axes), tiles.ndim))
    return tiles.reshape(-1, *value.shape)


def gathered_by_axis(value, axes, sequence, dim):
    return in_order(gather_in_order(value, axes, sequence), dim)


def sent_together(arrays, axis, split_dim, concat_dim, along):
    columns = [a.reshape(*a.shape[:along], -1) for a in arrays]
    both = jnp.concatenate(columns, axis=along)
    filled, at, gathered = (
        lax.all_to_all(both, axis, split_axis=split_dim, concat_axis=concat_dim, tiled=True),
        0,
        [],
    )
    for a, column in zip(arrays, columns):
        section = filled[..., at : at + column.shape[along]]
        gathered.append(section.reshape(*section.shape[:along], *a.shape[along:]))
        at += column.shape[along]
    return tuple(gathered)


def combine(former, latter):
    high_a, sums_a, weighted_a = former
    high_b, sums_b, weighted_b = latter
    highest = jnp.maximum(high_a, high_b)
    factor_a = jnp.exp(high_a - highest)
    factor_b = jnp.exp(high_b - highest)
    return (
        highest,
        sums_a * factor_a + sums_b * factor_b,
        weighted_a * factor_a[..., None] + weighted_b * factor_b[..., None],
    )


def fresh_term(query_rows, key_rows, value_rows, depth_pos, scaling):
    scores = (
        jnp.einsum("nd,ntd->nt", query_rows, key_rows, preferred_element_type=jnp.float32) * scaling
    )
    allowed = jnp.arange(key_rows.shape[1], dtype=jnp.int32)[None, :] <= depth_pos[:, None]
    highest = jnp.max(jnp.where(allowed, scores, FLOOR_SCORE), axis=1)
    weights = jnp.where(allowed, jnp.exp(scores - highest[:, None]), 0.0).astype(jnp.bfloat16)
    totals = jnp.sum(weights.astype(jnp.float32), axis=1)
    weighted = jnp.einsum("nt,ntd->nd", weights, value_rows, preferred_element_type=jnp.float32)
    return (highest, totals, weighted)


def on_device(queries, key_cache, value_cache, new_keys, new_values, chosen):
    page_count, page_tokens, head_span = key_cache.shape
    chosen_all = gathered_by_axis(chosen, PAGE, (1, 0, 2), 1)
    kv_heads = chosen_all.shape[0]
    head_width = head_span // kv_heads
    drafts = queries.shape[0]
    groups = queries.shape[1] // head_span
    row_count = drafts * groups
    scaling = head_width ** (-0.5)
    query_heads = (
        queries.reshape(drafts, kv_heads, groups, head_width)
        .transpose(1, 0, 2, 3)
        .reshape(kv_heads, row_count, head_width)
    )
    local_pages = chosen_all - lax.axis_index(PAGE) * page_count
    page_slots = jnp.arange(page_count, dtype=jnp.int32)
    picked = jnp.any(local_pages[:, :, None] == page_slots[None, None, :], axis=1)
    key_flat = key_cache.reshape(page_count * page_tokens, kv_heads, head_width)
    value_flat = value_cache.reshape(page_count * page_tokens, kv_heads, head_width)
    usable = jnp.repeat(picked, page_tokens, axis=1)
    scores = (
        jnp.einsum("hrd,nhd->hrn", query_heads, key_flat, preferred_element_type=jnp.float32)
        * scaling
    )
    scores = jnp.where(usable[:, None, :], scores, FLOOR_SCORE)
    highest = jnp.max(scores, axis=2)
    present = highest > 0.5 * FLOOR_SCORE
    offset = jnp.where(present, highest, 0.0)
    weights = jnp.where(usable[:, None, :], jnp.exp(scores - offset[..., None]), 0.0).astype(
        jnp.bfloat16
    )
    totals = jnp.sum(weights.astype(jnp.float32), axis=2)
    weighted = jnp.einsum("hrn,nhd->hrd", weights, value_flat, preferred_element_type=jnp.float32)
    all_rows = kv_heads * row_count
    highest = highest.reshape(all_rows)
    totals = totals.reshape(all_rows)
    weighted = weighted.reshape(all_rows, head_width)
    key_heads = new_keys.reshape(drafts, kv_heads, head_width).transpose(1, 0, 2)
    value_heads = new_values.reshape(drafts, kv_heads, head_width).transpose(1, 0, 2)
    query_flat = query_heads.reshape(all_rows, head_width)
    devices = lax.axis_size(PAGE)
    share_rows = all_rows // devices
    pieces = (
        highest.reshape(devices, share_rows),
        totals.reshape(devices, share_rows),
        weighted.reshape(devices, share_rows, head_width),
    )
    high_in, sums_in, weighted_in = sent_together((pieces[0], pieces[1], pieces[2]), PAGE, 0, 0, 2)
    merged_high = jnp.max(high_in, axis=0)
    factors = jnp.exp(high_in - merged_high[None, :])
    merged = (
        merged_high,
        jnp.sum(sums_in * factors, axis=0),
        jnp.sum(weighted_in * factors[..., None], axis=0),
    )
    first_row = lax.axis_index(PAGE) * share_rows
    row_ids = first_row + jnp.arange(share_rows, dtype=jnp.int32)
    query_own = lax.dynamic_slice_in_dim(query_flat, first_row, share_rows, 0)
    head_ids = row_ids // row_count
    depth_pos = row_ids % row_count // groups
    fresh = fresh_term(query_own, key_heads[head_ids], value_heads[head_ids], depth_pos, scaling)
    final_high, final_sums, final_weighted = combine(merged, fresh)
    finished = (final_weighted / final_sums[:, None]).astype(jnp.bfloat16)
    result = gathered_by_axis(finished, PAGE, (0, 1, 2), 0)
    return (
        result.reshape(kv_heads, drafts, groups, head_width)
        .transpose(1, 0, 2, 3)
        .reshape(drafts, kv_heads * groups * head_width)
    )


def solution(mesh):
    torus = Mesh(
        mesh.devices.reshape(mesh.shape["grp"], 16, 4, 2), ("grp", "page_0", "page_1", "page_2")
    )
    in_specs = (
        P("grp", None),
        P(GRP_PAGE, None, None),
        P(GRP_PAGE, None, None),
        P("grp", None),
        P("grp", None),
        P("grp", PAGE),
    )
    out_specs = P("grp", None)
    return jax.shard_map(
        on_device, mesh=torus, in_specs=in_specs, out_specs=out_specs, check_vma=False
    )
```

profile of v0, /device:TPU:33, one launch (start us, length us, event | category | flops | bytes accessed | tf_op | source)
XLA Modules:
  0.0 165.2 jit_solution(3029685596664027520)
XLA Ops:
  0.0 9.3 %all-gather.6 = s32[4,8,2]{1,2,0:T(2,128)S(1)} all-gather(s32[1,8,2]{1,2,0:T(2,128)} %bitcast.87), channel_id=2, replica_groups=mesh['grp'=2,'page_0'=16,'page_1'=4,'page_2'=2] {'page_1'}, dimensions={0}, use_global_device_ids=true | all-gather | bytes 320 | tf_op jit(solution)/shard_map/all_gather | solution.py:23
  9.3 41.4 %all-gather.1 = s32[64,8,2]{1,2,0:T(2,128)S(1)} all-gather(s32[4,8,2]{1,2,0:T(2,128)S(1)} %all-gather.6), channel_id=3, replica_groups=mesh['grp'=2,'page_0'=16,'page_1'=4,'page_2'=2] {'page_0'}, dimensions={0}, use_global_device_ids=true | all-gather | bytes 4352 | tf_op jit(solution)/shard_map/all_gather | solution.py:23
  50.7 11.5 %all-gather.2 = s32[32,4,8,2]{2,1,3,0:T(4,128)S(1)} all-gather(s32[16,4,8,2]{2,1,3,0:T(4,128)S(1)} %copy.132), channel_id=4, replica_groups=mesh['grp'=2,'page_0'=16,'page_1'=4,'page_2'=2] {'page_2'}, dimensions={0}, use_global_device_ids=true | all-gather | bytes 12288 | tf_op jit(solution)/shard_map/all_gather | solution.py:23
  62.7 0.2 fusion.6
  63.2 1.0 reshape.163
  64.2 3.3 %copy.163 = bf16[256,8,8,128]{3,2,1,0:T(8,128)(2,1)S(1)} copy(bf16[256,8,8,128]{3,1,2,0:T(8,128)(2,1)} %bitcast.71) | data formatting | bytes 8388608
  67.5 3.6 %fusion.4 = (f32[8,64]{1,0:T(8,128)S(1)}, f32[8,64,2048]{2,1,0:T(8,128)}) fusion(pred[8,2048]{1,0:T(8,128)(4,1)S(1)} %broadcast_in_dim.48, bf16[8,64,128]{2,1,0:T(8,128)(2,1)S(1)} %bitcast.74, bf16[2048,8,128]{2,1,0:T(8,128)(2,1)S(1)} %bitcast.70), kind=kOutput, calls=%fused_computation.9 | convolution fusion | flops 271580672 | bytes 8538112 | tf_op jit(solution)/shard_map/hrd,nhd->hrn/dot_general | solution.py:95
  71.1 0.3 reshape_reshape_reshape.12
  71.4 3.5 %convert_reduce_fusion = f32[8,64]{1,0:T(8,128)S(1)} fusion(f32[8,64]{1,0:T(8,128)S(1)} %compare_select_fusion, f32[8,64,2048]{2,1,0:T(8,128)} %get-tuple-element.14, pred[8,2048]{1,0:T(8,128)(4,1)S(1)} %broadcast_in_dim.48), kind=kLoop, calls=%fused_computation.6 | loop fusion | flops 7339520 | bytes 4214784 | tf_op jit(solution)/shard_map/reduce_sum | solution.py:105
  74.9 0.3 reshape_reshape_reshape.13
  75.3 3.5 %copy.164 = bf16[256,8,8,128]{3,2,1,0:T(8,128)(2,1)S(1)} copy(bf16[256,8,8,128]{3,1,2,0:T(8,128)(2,1)} %bitcast.72) | data formatting | bytes 8388608
  78.8 1.8 %fusion = f32[8,64,128]{2,1,0:T(8,128)S(1)} fusion(bf16[2048,8,128]{2,1,0:T(8,128)(2,1)S(1)} %bitcast.73, f32[8,64,2048]{2,1,0:T(8,128)S(1)} %copy-done.1, f32[8,64]{1,0:T(8,128)S(1)} %compare_select_fusion, pred[8,2048]{1,0:T(8,128)(4,1)S(1)} %broadcast_in_dim.48), kind=kOutput, calls=%fused_computation.2 | convolution fusion | flops 273678336 | bytes 8669184 | tf_op jit(solution)/shard_map/hrn,nhd->hrd/dot_general | solution.py:106
  80.5 1.4 pad_maximum_fusion
  81.9 7.6 %all-to-all-start = ((f32[128,4,130]{2,1,0:T(4,128)}), f32[128,4,130]{2,1,0:T(4,128)S(1)}, u32[]{:S(2)}, u32[]{:S(2)}) async-start(f32[128,4,130]{2,1,0:T(4,128)} %pad_maximum_fusion), calls=%async_computation | async-start | bytes 1048576 | tf_op jit(solution)/shard_map/all_to_all | solution.py:38
  89.7 0.6 gather_fusion
  90.2 0.6 gather_fusion.1
  91.5 29.0 %all-to-all-done = f32[128,4,130]{2,1,0:T(4,128)S(1)} async-done(((f32[128,4,130]{2,1,0:T(4,128)}), f32[128,4,130]{2,1,0:T(4,128)S(1)}, u32[]{:S(2)}, u32[]{:S(2)}) %all-to-all-start) | async-done | bytes 266272 | tf_op jit(solution)/shard_map/all_to_all | solution.py:38
  120.5 0.3 slice_reduce_fusion
  121.2 0.2 fusion.9
  121.4 0.3 fusion.5
  121.9 21.8 %all-gather.7 = bf16[16,4,128]{2,1,0:T(4,128)(2,1)S(1)} all-gather(bf16[1,4,128]{2,1,0:T(4,128)(2,1)S(1)} %fusion.15), channel_id=5, replica_groups=mesh['grp'=2,'page_0'=16,'page_1'=4,'page_2'=2] {'page_0'}, dimensions={0}, use_global_device_ids=true | all-gather | bytes 17408 | tf_op jit(solution)/shard_map/all_gather | solution.py:23
  143.6 9.1 %all-gather.4 = bf16[64,4,128]{2,1,0:T(4,128)(2,1)S(1)} all-gather(bf16[16,4,128]{2,1,0:T(4,128)(2,1)S(1)} %all-gather.7), channel_id=6, replica_groups=mesh['grp'=2,'page_0'=16,'page_1'=4,'page_2'=2] {'page_1'}, dimensions={0}, use_global_device_ids=true | all-gather | bytes 81920 | tf_op jit(solution)/shard_map/all_gather | solution.py:23
  152.7 11.5 %all-gather.5 = bf16[8,16,4,128]{3,1,0,2:T(8,128)(2,1)S(1)} all-gather(bf16[4,16,4,128]{3,1,0,2:T(8,128)(2,1)S(1)} %bitcast.82), channel_id=7, replica_groups=mesh['grp'=2,'page_0'=16,'page_1'=4,'page_2'=2] {'page_2'}, dimensions={0}, use_global_device_ids=true | all-gather | bytes 196608 | tf_op jit(solution)/shard_map/all_gather | solution.py:23
  164.5 0.7 reshape.171
  (36 shorter events, 2.3 us)
Async XLA Ops:
  0.0 89.6 %copy-start = (bf16[16,1024]{1,0:T(8,128)(2,1)S(1)}, bf16[16,1024]{1,0:T(8,128)(2,1)}, u32[]{:S(2)}) copy-start(bf16[16,1024]{1,0:T(8,128)(2,1)} %param.9) | copy-start | bytes 98308
  75.3 3.5 %copy-start.1 = (f32[8,64,2048]{2,1,0:T(8,128)S(1)}, f32[8,64,2048]{2,1,0:T(8,128)}, u32[]{:S(2)}) copy-start(f32[8,64,2048]{2,1,0:T(8,128)} %get-tuple-element.14) | copy-start | bytes 12582916
  78.8 10.9 %copy-start.2 = (bf16[16,1024]{1,0:T(8,128)(2,1)S(1)}, bf16[16,1024]{1,0:T(8,128)(2,1)}, u32[]{:S(2)}) copy-start(bf16[16,1024]{1,0:T(8,128)(2,1)} %param.10) | copy-start | bytes 98308
  81.9 38.5 %all-to-all-start = ((f32[128,4,130]{2,1,0:T(4,128)}), f32[128,4,130]{2,1,0:T(4,128)S(1)}, u32[]{:S(2)}, u32[]{:S(2)}) async-start(f32[128,4,130]{2,1,0:T(4,128)} %pad_maximum_fusion), calls=%async_computation | async-start | bytes 1048576 | tf_op jit(solution)/shard_map/all_to_all | solution.py:38
where the time goes:
time: 166 us; the launch traced here: 165 us
  blocking collectives  105 us (63%)
  waiting for transfers between devices  29 us (17%)
  local copies, waits for them, and re-layouts  11.6 us (7%)
  starting transfers between devices  7.63 us (5%)
  other arithmetic  6.58 us (4%)
  matrix products  5.59 us (3%)
    all_gather x6, blocking collectives, gather_in_order(): tiles = lax.all_gather(tiles, axes[k])  105 us
    all_to_all x1, waiting for transfers between devices, sent_together(): lax.all_to_all(both, axis, split_axis=split_dim, concat_axis=concat_dim,...  29 us
    all_to_all x1, starting transfers between devices, sent_together(): lax.all_to_all(both, axis, split_axis=split_dim, concat_axis=concat_dim,...  7.63 us
    unnamed x9, local copies, waits for them, and re-layouts  6.86 us
    dot_general x1, matrix products, on_device(): jnp.einsum('hrd,nhd->hrn', query_heads, key_flat, preferred_element_type=...  3.6 us
    reduce_sum x1, other arithmetic, on_device(): totals = jnp.sum(weights.astype(jnp.float32), axis=2)  3.5 us
  transfers between devices with their start and end apart: 1, of which 1 were waited for; matrix products, arithmetic and copies ran while one was open for 1% of the time, Pallas kernels for 0%

commit v1 on v0

v1 whole, which is shorter than its diff:
```python
import jax
import jax.numpy as jnp
from jax import lax
from jax.experimental import pallas as pl
from jax.experimental.pallas import tpu as pltpu
from jax.sharding import Mesh
from jax.sharding import PartitionSpec as P

GRP_PAGE = ("grp", "page_0", "page_1", "page_2")
PAGE = GRP_PAGE[1:]
FLOOR = -1e30
F32 = jnp.float32
BF16 = jnp.bfloat16
MESH = pl.DeviceIdType.MESH


def dot_nt(a, b):
    return lax.dot_general(a, b, (((1,), (1,)), ((), ())), preferred_element_type=F32)


def dot_nn(a, b):
    return lax.dot_general(a, b, (((1,), (0,)), ((), ())), preferred_element_type=F32)


def rows_of(ref, count):
    return jnp.concatenate([ref[i] for i in range(count)], axis=0)


def flip(x):
    n = x.shape[0]
    if n < 128:
        x = jnp.concatenate([x, jnp.zeros((128 - n, 128), x.dtype)], axis=0)
    return jnp.transpose(x)


def merge_weights(lse):
    top = jnp.max(lse, axis=0, keepdims=True)
    w = jnp.exp(lse - top)
    total = jnp.sum(w, axis=0, keepdims=True)
    return w / total, top + jnp.log(total)


def far_first(n, ring):
    def key(d):
        return -min(d // ring, (n - d) // ring)

    return sorted(range(1, n), key=key)


def make_kernel(nz, nx, nc, heads, tokens, page_tokens, drafts, groups, scaling):
    na = nx * nc * 2
    nb = nz // 2
    pages = tokens // page_tokens
    block_rows = heads * groups * drafts // na
    per_head = na // heads
    width = block_rows // drafts * 128

    def kernel(
        q_ref, ids_ref, nk_ref, nv_ref, k_hbm, v_hbm, out_ref,
        ks, vs, s_ref, idbs, idbr, idas, idar,
        o1s, l1s, o1r, l1r, o2s, l2s, o2r, l2r, fs, fr, msc, ex,
        k_sem, v_sem, b_send, b_recv, a_send, a_recv,
        o1_send, o1_recv, l1_send, l1_recv,
        o2_send, o2_recv, l2_send, l2_recv, f_send, f_recv,
    ):
        z = lax.axis_index("page_0")
        x = lax.axis_index("page_1")
        c = lax.axis_index("page_2")
        zlow = lax.rem(z, 2)
        b = lax.div(z, 2)
        a = (x * nc + c) * 2 + zlow

        def a_dev(d):
            t = lax.rem(a + d, na)
            u = lax.div(t, 2)
            return t, {
                "page_0": b * 2 + lax.rem(t, 2),
                "page_1": lax.div(u, nc),
                "page_2": lax.rem(u, nc),
            }

        def b_dev(d):
            t = lax.rem(b + d, nb)
            return t, {"page_0": t * 2 + zlow, "page_1": x, "page_2": c}

        order_a = far_first(na, nc * 2)
        order_b = far_first(nb, 1)

        def copy(src, dst, ss, rs, dev):
            return pltpu.make_async_remote_copy(
                src_ref=src, dst_ref=dst, send_sem=ss, recv_sem=rs,
                device_id=dev, device_id_type=MESH,
            )

        def send(group, order, src, dst, me, ss, rs):
            started = []
            for d in order:
                t, dev = group(d)
                r = copy(src(t), dst.at[me], ss.at[d], rs.at[me], dev)
                r.start()
                started.append(r)
            return started

        def wait_all(group, order, src, dst, n, ss, rs):
            for d in order[::-1]:
                t, dev = group(n - d)
                copy(src(t), dst.at[t], ss.at[n - d], rs.at[t], dev).wait_recv()

        barrier = pltpu.get_barrier_semaphore()
        for d in order_b:
            pl.semaphore_signal(barrier, inc=1, device_id=b_dev(d)[1], device_id_type=MESH)
        for d in order_a:
            pl.semaphore_signal(barrier, inc=1, device_id=a_dev(d)[1], device_id_type=MESH)

        def load(src, dst, sem, h):
            return pltpu.make_async_copy(src.at[:, pl.ds(h * 128, 128)], dst.at[h], sem.at[h])

        for h in range(heads):
            load(k_hbm, ks, k_sem, h).start()
        for h in range(heads):
            load(v_hbm, vs, v_sem, h).start()

        lane = lax.broadcasted_iota(jnp.int32, (1, 128), 1)
        slot = 128 // nb
        idbs[...] = jnp.where(lax.div(lane, slot) == b, ids_ref[...], 0)
        idbr[b] = idbs[...]

        def scores(h):
            load(k_hbm, ks, k_sem, h).wait()
            base = h * groups * 128
            q = jnp.concatenate(
                [q_ref[:, base + g * 128 : base + (g + 1) * 128] for g in range(groups)], axis=0
            )
            s_ref[h] = dot_nt(q, ks[h]) * scaling

        half = heads // 2
        for h in range(half):
            scores(h)

        cols = pl.multiple_of(a * width, width)
        head_cols = pl.multiple_of(lax.div(a, per_head) * 128, 128)
        q_own = q_ref[:, pl.ds(cols, width)]
        q_own = jnp.concatenate(
            [q_own[:, i * 128 : (i + 1) * 128] for i in range(width // 128)], axis=0
        )
        pad = jnp.zeros((128 - drafts, 128), BF16)
        kf = jnp.concatenate([nk_ref[:, pl.ds(head_cols, 128)], pad], axis=0)
        vf = jnp.concatenate([nv_ref[:, pl.ds(head_cols, 128)], pad], axis=0)
        sf = dot_nt(q_own, kf) * scaling
        pos = lax.rem(lax.broadcasted_iota(jnp.int32, sf.shape, 0), drafts)
        ok = lax.broadcasted_iota(jnp.int32, sf.shape, 1) <= pos
        sf = jnp.where(ok, sf, FLOOR)
        mf = jnp.max(sf, axis=1, keepdims=True)
        pf = jnp.where(ok, jnp.exp(sf - mf), 0.0).astype(BF16)
        tf = jnp.sum(pf.astype(F32), axis=1, keepdims=True)
        of = dot_nn(pf, vf) / tf
        lf = flip(jnp.broadcast_to(mf + jnp.log(tf), (block_rows, 128)))[0:1]

        key_page = lax.div(lax.broadcasted_iota(jnp.int32, (128, tokens), 1), page_tokens)
        row_page = lax.broadcasted_iota(jnp.int32, (128, tokens), 0)
        ex[...] = (key_page == row_page).astype(F32).astype(BF16)

        pl.semaphore_wait(barrier, na - 1 + nb - 1)
        sent = send(b_dev, order_b, lambda t: idbs, idbr, b, b_send, b_recv)
        for h in range(half, heads):
            scores(h)
        wait_all(b_dev, order_b, lambda t: idbs, idbr, nb, b_send, b_recv)
        joined = idbr[0]
        for i in range(1, nb):
            joined = joined + idbr[i]
        idas[...] = joined
        idar[a] = joined
        sent += send(a_dev, order_a, lambda t: idas, idar, a, a_send, a_recv)
        for h in range(heads):
            load(v_hbm, vs, v_sem, h).wait()
        wait_all(a_dev, order_a, lambda t: idas, idar, na, a_send, a_recv)

        local = rows_of(idar, na) - ((z * nx + x) * nc + c) * pages
        counts = [
            jnp.sum((local == p).astype(F32), axis=0, keepdims=True) for p in range(pages)
        ]
        counts.append(jnp.zeros((128 - pages, 128), F32))
        counts = jnp.concatenate(counts, axis=0).astype(BF16)
        lane_head = lax.div(lax.rem(lax.broadcasted_iota(jnp.int32, (heads, 128), 1), slot), slot // heads)
        pick = (lane_head == lax.broadcasted_iota(jnp.int32, (heads, 128), 0)).astype(F32).astype(BF16)
        picked = dot_nt(pick, counts).astype(BF16)
        usable = dot_nn(picked, ex[...])

        lanes = lax.broadcasted_iota(jnp.int32, (block_rows, 128), 1)
        stats = jnp.zeros((block_rows, 128), F32)
        for h in range(heads):
            s = jnp.where(usable[h : h + 1] > 0.5, s_ref[h], FLOOR)
            top = jnp.max(s, axis=1, keepdims=True)
            offset = jnp.where(top > 0.5 * FLOOR, top, 0.0)
            p = jnp.exp(s - offset).astype(BF16)
            total = jnp.sum(p.astype(F32), axis=1, keepdims=True)
            safe = jnp.maximum(total, 0.5)
            o = dot_nn(p, vs[h]) / safe
            lse = jnp.where(total > 0.0, offset + jnp.log(safe), FLOOR)
            for i in range(per_head):
                part = slice(i * block_rows, (i + 1) * block_rows)
                o1s[h * per_head + i] = o[part].astype(BF16)
                stats = jnp.where(lanes == h * per_head + i, lse[part], stats)
        stats = flip(stats)
        for i in range(na):
            l1s[i] = stats[i : i + 1]
        l1r[a] = l1s[a]
        o1r[a] = o1s[a]
        sent += send(a_dev, order_a, lambda t: l1s.at[t], l1r, a, l1_send, l1_recv)
        sent += send(a_dev, order_a, lambda t: o1s.at[t], o1r, a, o1_send, o1_recv)
        wait_all(a_dev, order_a, lambda t: l1s.at[t], l1r, na, l1_send, l1_recv)
        w, lse = merge_weights(rows_of(l1r, na))
        w = flip(w)[0:block_rows]
        l2s[...] = lse
        l2r[b] = lse
        sent += send(b_dev, order_b, lambda t: l2s, l2r, b, l2_send, l2_recv)
        wait_all(a_dev, order_a, lambda t: o1s.at[t], o1r, na, o1_send, o1_recv)
        o = w[:, 0:1] * o1r[0].astype(F32)
        for i in range(1, na):
            o = o + w[:, i : i + 1] * o1r[i].astype(F32)
        o = o.astype(BF16)
        o2s[...] = o
        o2r[b] = o
        sent += send(b_dev, order_b, lambda t: o2s, o2r, b, o2_send, o2_recv)
        wait_all(b_dev, order_b, lambda t: l2s, l2r, nb, l2_send, l2_recv)
        w, _ = merge_weights(jnp.concatenate([lf, rows_of(l2r, nb)], axis=0))
        w = flip(w)[0:block_rows]
        o = w[:, 0:1] * of
        wait_all(b_dev, order_b, lambda t: o2s, o2r, nb, o2_send, o2_recv)
        for i in range(nb):
            o = o + w[:, i + 1 : i + 2] * o2r[i].astype(F32)
        o = o.astype(BF16)
        block = jnp.concatenate(
            [o[i * drafts : (i + 1) * drafts] for i in range(width // 128)], axis=1
        )
        fs[...] = block
        fr[a] = block
        sent += send(a_dev, order_a, lambda t: fs, fr, a, f_send, f_recv)
        wait_all(a_dev, order_a, lambda t: fs, fr, na, f_send, f_recv)
        for i in range(na):
            out_ref[:, i * width : (i + 1) * width] = fr[i]
        for r in sent:
            r.wait_send()

    dma = pltpu.SemaphoreType.DMA
    span = heads * 128
    rows = heads * groups * drafts // heads
    scratch = [
        pltpu.VMEM((heads, tokens, 128), BF16),
        pltpu.VMEM((heads, tokens, 128), BF16),
        pltpu.VMEM((heads, rows, tokens), F32),
        pltpu.VMEM((1, 128), jnp.int32),
        pltpu.VMEM((nb, 1, 128), jnp.int32),
        pltpu.VMEM((1, 128), jnp.int32),
        pltpu.VMEM((na, 1, 128), jnp.int32),
        pltpu.VMEM((na, block_rows, 128), BF16),
        pltpu.VMEM((na, 1, 128), F32),
        pltpu.VMEM((na, block_rows, 128), BF16),
        pltpu.VMEM((na, 1, 128), F32),
        pltpu.VMEM((block_rows, 128), BF16),
        pltpu.VMEM((1, 128), F32),
        pltpu.VMEM((nb, block_rows, 128), BF16),
        pltpu.VMEM((nb, 1, 128), F32),
        pltpu.VMEM((drafts, width), BF16),
        pltpu.VMEM((na, drafts, width), BF16),
        pltpu.VMEM((block_rows, 128), F32),
        pltpu.VMEM((128, tokens), BF16),
        dma((heads,)), dma((heads,)),
        dma((nb,)), dma((nb,)), dma((na,)), dma((na,)),
        dma((na,)), dma((na,)), dma((na,)), dma((na,)),
        dma((nb,)), dma((nb,)), dma((nb,)), dma((nb,)), dma((na,)), dma((na,)),
    ]
    vmem = pl.BlockSpec(memory_space=pltpu.VMEM)
    anyspace = pl.BlockSpec(memory_space=pl.ANY)
    return pl.pallas_call(
        kernel,
        out_shape=jax.ShapeDtypeStruct((drafts, heads * groups * 128), BF16),
        in_specs=[vmem, vmem, vmem, vmem, anyspace, anyspace],
        out_specs=vmem,
        scratch_shapes=scratch,
        compiler_params=pltpu.CompilerParams(
            collective_id=0, has_side_effects=True, vmem_limit_bytes=48 * 1024 * 1024
        ),
    )


def solution(mesh):
    nz, nx, nc = 16, 4, 2
    torus = Mesh(
        mesh.devices.reshape(mesh.shape["grp"], nz, nx, nc), ("grp", "page_0", "page_1", "page_2")
    )

    def on_device(queries, key_cache, value_cache, new_keys, new_values, chosen):
        pages, page_tokens, span = key_cache.shape
        heads = chosen.shape[0]
        drafts = queries.shape[0]
        groups = queries.shape[1] // span
        call = make_kernel(
            nz, nx, nc, heads, pages * page_tokens, page_tokens, drafts, groups,
            (span // heads) ** (-0.5),
        )
        ids = jnp.tile(chosen.reshape(1, -1), (1, 128 // chosen.size))
        return call(
            queries, ids, new_keys, new_values,
            key_cache.reshape(-1, span), value_cache.reshape(-1, span),
        )

    in_specs = (
        P("grp", None),
        P(GRP_PAGE, None, None),
        P(GRP_PAGE, None, None),
        P("grp", None),
        P("grp", None),
        P("grp", PAGE),
    )
    return jax.shard_map(
        on_device, mesh=torus, in_specs=in_specs, out_specs=P("grp", None), check_vma=False
    )
```

time: 166 us -> 64.4 us (0.39)
  blocking collectives: 105 us -> 0 us
  Pallas kernels: 0 us -> 57.9 us
  waiting for transfers between devices: 29 us -> 0 us
  starting transfers between devices: 7.63 us -> 0 us
  other arithmetic: 6.58 us -> 0 us
  matrix products: 5.59 us -> 0 us
  local copies, waits for them, and re-layouts: 11.6 us -> 6.19 us
    all_gather x6 -> x0, blocking collectives: 105 us -> none  [gather_in_order(): tiles = lax.all_gather(tiles, axes[k])]
    pallas_call x0 -> x1, Pallas kernels: none -> 57.9 us  [on_device(): call(queries, ids, new_keys, new_values, key_cache.reshape(-1, span), val...]
    all_to_all x1 -> x0, waiting for transfers between devices: 29 us -> none  [sent_together(): lax.all_to_all(both, axis, split_axis=split_dim, concat_axis=concat_dim,...]
    all_to_all x1 -> x0, starting transfers between devices: 7.63 us -> none  [sent_together(): lax.all_to_all(both, axis, split_axis=split_dim, concat_axis=concat_dim,...]
    dot_general x4 -> x0, matrix products: 5.59 us -> none  [the longest x1 3.6 us: on_device(): jnp.einsum('hrd,nhd->hrn', query_heads, key_flat, preferred_element_type=...]
    reduce_sum x4 -> x0, other arithmetic: 4.24 us -> none  [the longest x1 3.5 us: on_device(): totals = jnp.sum(weights.astype(jnp.float32), axis=2)]
    reshape x3 -> x0, local copies, waits for them, and re-layouts: 1.75 us -> none  [the longest x2 1.02 us: on_device(): queries.reshape(drafts, kv_heads, groups, head_width).transpose(1, 0, 2, 3)]
    unnamed x9 -> x10, local copies, waits for them, and re-layouts: 6.86 us -> 6.02 us
  transfers between devices with their start and end apart: 1 -> 0, of which waited for: 1 -> 0; matrix products, arithmetic and copies ran while one was open for 1% -> 0% of each run, Pallas kernels for 0% -> 0%
where the time goes in v1:
time: 64.4 us; the launch traced here: 64.1 us
  Pallas kernels  57.9 us (90%)
  local copies, waits for them, and re-layouts  6.19 us (10%)
    pallas_call x1, Pallas kernels, on_device(): call(queries, ids, new_keys, new_values, key_cache.reshape(-1, span), val...  57.9 us
    unnamed x10, local copies, waits for them, and re-layouts  6.02 us

profile of v1, /device:TPU:33, one launch (start us, length us, event | category | flops | bytes accessed | tf_op | source)
XLA Modules:
  0.0 64.1 jit_solution(17565505837336119917)
XLA Ops:
  0.0 0.8 %copy.8 = s32[8,2]{1,0:T(8,128)S(1)} copy(s32[8,2]{0,1:T(2,128)} %param.11) | data formatting | bytes 128 | tf_op args[5]
  0.8 0.1 tile.10
  0.8 0.1 tile.12.ids_ref
  0.9 0.0 copy-start
  0.9 2.2 %copy-done = bf16[32,64,1024]{2,1,0:T(8,128)(2,1)S(1)} copy-done((bf16[32,64,1024]{2,1,0:T(8,128)(2,1)S(1)}, bf16[32,64,1024]{2,1,0:T(8,128)(2,1)}, u32[]{:S(2)}) %copy-start) | copy-done | bytes 4194328
  3.1 0.0 copy-start.1
  3.1 0.9 %copy-done.1 = bf16[16,4096]{1,0:T(8,128)(2,1)S(1)} copy-done((bf16[16,4096]{1,0:T(8,128)(2,1)S(1)}, bf16[16,4096]{1,0:T(8,128)(2,1)}, u32[]{:S(2)}) %copy-start.1) | copy-done | bytes 131096
  4.0 0.0 copy-start.2
  4.0 0.8 %copy-done.2 = bf16[16,1024]{1,0:T(8,128)(2,1)S(1)} copy-done((bf16[16,1024]{1,0:T(8,128)(2,1)S(1)}, bf16[16,1024]{1,0:T(8,128)(2,1)}, u32[]{:S(2)}) %copy-start.2) | copy-done | bytes 32792
  4.8 0.0 copy-start.3
  4.8 0.8 %copy-done.3 = bf16[16,1024]{1,0:T(8,128)(2,1)S(1)} copy-done((bf16[16,1024]{1,0:T(8,128)(2,1)S(1)}, bf16[16,1024]{1,0:T(8,128)(2,1)}, u32[]{:S(2)}) %copy-start.3) | copy-done | bytes 32792
  5.5 57.9 %shard_map.64 = bf16[16,4096]{1,0:T(8,128)(2,1)S(1)} custom-call(bf16[16,4096]{1,0:T(8,128)(2,1)S(1)} %copy-done.1, s32[1,128]{1,0:T(1,128)S(1)} %tile.12.ids_ref, bf16[16,1024]{1,0:T(8,128)(2,1)S(1)} %copy-done.2, bf16[16,1024]{1,0:T(8,128)(2,1)S(1)} %copy-done.3, bf16[2048,1024]{1,0:T(8,128)(2,1)S(1)} %bitcast.2, bf16[2048,1024]{1,0:T(8,128)(2,1)} %bitcast.3), custom_call_target="tpu_custom_call" | custom-call | tf_op jit(solution)/shard_map/pallas_call | solution.py:303
  63.4 0.7 %copy.10 = bf16[16,4096]{1,0:T(8,128)(2,1)} copy(bf16[16,4096]{1,0:T(8,128)(2,1)S(1)} %shard_map.64) | data formatting | bytes 262144
  (1 shorter events, 0.0 us)
Async XLA Ops:
  0.9 2.2 %copy-start = (bf16[32,64,1024]{2,1,0:T(8,128)(2,1)S(1)}, bf16[32,64,1024]{2,1,0:T(8,128)(2,1)}, u32[]{:S(2)}) copy-start(bf16[32,64,1024]{2,1,0:T(8,128)(2,1)} %param.7) | copy-start | bytes 12582916
  3.1 0.9 %copy-start.1 = (bf16[16,4096]{1,0:T(8,128)(2,1)S(1)}, bf16[16,4096]{1,0:T(8,128)(2,1)}, u32[]{:S(2)}) copy-start(bf16[16,4096]{1,0:T(8,128)(2,1)} %q_ref.1) | copy-start | bytes 393220
  4.0 0.8 %copy-start.2 = (bf16[16,1024]{1,0:T(8,128)(2,1)S(1)}, bf16[16,1024]{1,0:T(8,128)(2,1)}, u32[]{:S(2)}) copy-start(bf16[16,1024]{1,0:T(8,128)(2,1)} %nk_ref.1) | copy-start | bytes 98308
  4.8 0.8 %copy-start.3 = (bf16[16,1024]{1,0:T(8,128)(2,1)S(1)}, bf16[16,1024]{1,0:T(8,128)(2,1)}, u32[]{:S(2)}) copy-start(bf16[16,1024]{1,0:T(8,128)(2,1)} %nv_ref.1) | copy-start | bytes 98308

commit v2 on v1

--- a/solution.py
+++ b/solution.py
@@ -56,9 +56,9 @@
     width = block_rows // drafts * 128
 
     def kernel(
-        q_ref, ids_ref, nk_ref, nv_ref, k_hbm, v_hbm, out_ref,
-        ks, vs, s_ref, idbs, idbr, idas, idar,
-        o1s, l1s, o1r, l1r, o2s, l2s, o2r, l2r, fs, fr, msc, ex,
+        q_hbm, ids_hbm, nk_hbm, nv_hbm, k_hbm, v_hbm, out_ref,
+        q_ref, ids_ref, nk_ref, nv_ref, small_sem, ks, vs, s_ref, idbs, idbr, idas, idar,
+        o1s, l1s, o1r, l1r, o2s, l2s, o2r, l2r, fs, fr, ex,
         k_sem, v_sem, b_send, b_recv, a_send, a_recv,
         o1_send, o1_recv, l1_send, l1_recv,
         o2_send, o2_recv, l2_send, l2_recv, f_send, f_recv,
@@ -106,6 +106,13 @@
                 t, dev = group(n - d)
                 copy(src(t), dst.at[t], ss.at[n - d], rs.at[t], dev).wait_recv()
 
+        small = [
+            pltpu.make_async_copy(src, dst, small_sem.at[i])
+            for i, (src, dst) in enumerate(
+                [(ids_hbm, ids_ref), (q_hbm, q_ref), (nk_hbm, nk_ref), (nv_hbm, nv_ref)]
+            )
+        ]
+        small[0].start()
         barrier = pltpu.get_barrier_semaphore()
         for d in order_b:
             pl.semaphore_signal(barrier, inc=1, device_id=b_dev(d)[1], device_id_type=MESH)
@@ -115,6 +122,8 @@
         def load(src, dst, sem, h):
             return pltpu.make_async_copy(src.at[:, pl.ds(h * 128, 128)], dst.at[h], sem.at[h])
 
+        for r in small[1:]:
+            r.start()
         for h in range(heads):
             load(k_hbm, ks, k_sem, h).start()
         for h in range(heads):
@@ -122,7 +131,10 @@
 
         lane = lax.broadcasted_iota(jnp.int32, (1, 128), 1)
         slot = 128 // nb
-        idbs[...] = jnp.where(lax.div(lane, slot) == b, ids_ref[...], 0)
+        small[0].wait()
+        ids = ids_ref[...]
+        ids = jnp.concatenate([ids[j : j + 1] for j in range(ids.shape[0])] * nb, axis=1)
+        idbs[...] = jnp.where(lax.div(lane, slot) == b, ids, 0)
         idbr[b] = idbs[...]
 
         def scores(h):
@@ -133,8 +145,11 @@
             )
             s_ref[h] = dot_nt(q, ks[h]) * scaling
 
-        half = heads // 2
-        for h in range(half):
+        pl.semaphore_wait(barrier, na - 1 + nb - 1)
+        sent = send(b_dev, order_b, lambda t: idbs, idbr, b, b_send, b_recv)
+        for r in small[1:]:
+            r.wait()
+        for h in range(heads):
             scores(h)
 
         cols = pl.multiple_of(a * width, width)
@@ -160,10 +175,6 @@
         row_page = lax.broadcasted_iota(jnp.int32, (128, tokens), 0)
         ex[...] = (key_page == row_page).astype(F32).astype(BF16)
 
-        pl.semaphore_wait(barrier, na - 1 + nb - 1)
-        sent = send(b_dev, order_b, lambda t: idbs, idbr, b, b_send, b_recv)
-        for h in range(half, heads):
-            scores(h)
         wait_all(b_dev, order_b, lambda t: idbs, idbr, nb, b_send, b_recv)
         joined = idbr[0]
         for i in range(1, nb):
@@ -181,7 +192,7 @@
         ]
         counts.append(jnp.zeros((128 - pages, 128), F32))
         counts = jnp.concatenate(counts, axis=0).astype(BF16)
-        lane_head = lax.div(lax.rem(lax.broadcasted_iota(jnp.int32, (heads, 128), 1), slot), slot // heads)
+        lane_head = lax.rem(lax.broadcasted_iota(jnp.int32, (heads, 128), 1), heads)
         pick = (lane_head == lax.broadcasted_iota(jnp.int32, (heads, 128), 0)).astype(F32).astype(BF16)
         picked = dot_nt(pick, counts).astype(BF16)
         usable = dot_nn(picked, ex[...])
@@ -246,6 +257,11 @@
     span = heads * 128
     rows = heads * groups * drafts // heads
     scratch = [
+        pltpu.VMEM((drafts, heads * groups * 128), BF16),
+        pltpu.VMEM((128 // nb // heads, heads), jnp.int32),
+        pltpu.VMEM((drafts, span), BF16),
+        pltpu.VMEM((drafts, span), BF16),
+        dma((4,)),
         pltpu.VMEM((heads, tokens, 128), BF16),
         pltpu.VMEM((heads, tokens, 128), BF16),
         pltpu.VMEM((heads, rows, tokens), F32),
@@ -263,7 +279,6 @@
         pltpu.VMEM((nb, 1, 128), F32),
         pltpu.VMEM((drafts, width), BF16),
         pltpu.VMEM((na, drafts, width), BF16),
-        pltpu.VMEM((block_rows, 128), F32),
         pltpu.VMEM((128, tokens), BF16),
         dma((heads,)), dma((heads,)),
         dma((nb,)), dma((nb,)), dma((na,)), dma((na,)),
@@ -271,15 +286,15 @@
         dma((nb,)), dma((nb,)), dma((nb,)), dma((nb,)), dma((na,)), dma((na,)),
     ]
     vmem = pl.BlockSpec(memory_space=pltpu.VMEM)
-    anyspace = pl.BlockSpec(memory_space=pl.ANY)
+    hbm = pl.BlockSpec(memory_space=pltpu.HBM)
     return pl.pallas_call(
         kernel,
         out_shape=jax.ShapeDtypeStruct((drafts, heads * groups * 128), BF16),
-        in_specs=[vmem, vmem, vmem, vmem, anyspace, anyspace],
+        in_specs=[hbm] * 6,
         out_specs=vmem,
         scratch_shapes=scratch,
         compiler_params=pltpu.CompilerParams(
-            collective_id=0, has_side_effects=True, vmem_limit_bytes=48 * 1024 * 1024
+            collective_id=0, has_side_effects=True, vmem_limit_bytes=60 * 1024 * 1024
         ),
     )
 
@@ -299,9 +314,8 @@
             nz, nx, nc, heads, pages * page_tokens, page_tokens, drafts, groups,
             (span // heads) ** (-0.5),
         )
-        ids = jnp.tile(chosen.reshape(1, -1), (1, 128 // chosen.size))
         return call(
-            queries, ids, new_keys, new_values,
+            queries, chosen.T, new_keys, new_values,
             key_cache.reshape(-1, span), value_cache.reshape(-1, span),
         )
 

time: 64.4 us -> 60.1 us (0.933)
  local copies, waits for them, and re-layouts: 6.19 us -> 1.57 us
    unnamed x10 -> x1, local copies, waits for them, and re-layouts: 6.02 us -> 1.57 us
where the time goes in v2:
time: 60.1 us; the launch traced here: 60 us
  Pallas kernels  58.4 us (97%)
  local copies, waits for them, and re-layouts  1.57 us (3%)
    pallas_call x1, Pallas kernels, on_device(): call(queries, chosen.T, new_keys, new_values, key_cache.reshape(-1, span)...  58.4 us
    unnamed x1, local copies, waits for them, and re-layouts  1.57 us

profile of v2, /device:TPU:33, one launch (start us, length us, event | category | flops | bytes accessed | tf_op | source)
XLA Modules:
  0.0 60.0 jit_solution(15354819049642441111)
XLA Ops:
  0.0 58.4 %shard_map.64 = bf16[16,4096]{1,0:T(8,128)(2,1)} custom-call(bf16[16,4096]{1,0:T(8,128)(2,1)} %q_hbm.1, s32[2,8]{1,0:T(2,128)} %bitcast.5, bf16[16,1024]{1,0:T(8,128)(2,1)} %nk_hbm.1, bf16[16,1024]{1,0:T(8,128)(2,1)} %nv_hbm.1, bf16[2048,1024]{1,0:T(8,128)(2,1)} %bitcast.3, bf16[2048,1024]{1,0:T(8,128)(2,1)} %bitcast.4), custom_call_target="tpu_custom_call" | custom-call | tf_op jit(solution)/shard_map/pallas_call | solution.py:317
  58.4 1.6 %copy.8 = bf16[16,4096]{1,0:T(8,128)(2,1)} copy(bf16[16,4096]{1,0:T(8,128)(2,1)} %shard_map.64) | data formatting | bytes 262144

commit v3 on v2

--- a/solution.py
+++ b/solution.py
@@ -58,7 +58,7 @@
     def kernel(
         q_hbm, ids_hbm, nk_hbm, nv_hbm, k_hbm, v_hbm, out_ref,
         q_ref, ids_ref, nk_ref, nv_ref, small_sem, ks, vs, s_ref, idbs, idbr, idas, idar,
-        o1s, l1s, o1r, l1r, o2s, l2s, o2r, l2r, fs, fr, ex,
+        o1s, l1s, o1r, l1r, o2s, l2s, o2r, l2r, fs, fr, ex, us,
         k_sem, v_sem, b_send, b_recv, a_send, a_recv,
         o1_send, o1_recv, l1_send, l1_recv,
         o2_send, o2_recv, l2_send, l2_recv, f_send, f_recv,
@@ -113,6 +113,16 @@
             )
         ]
         small[0].start()
+        def send_pairs(src, dst, ss, rs):
+            for t in range(nb):
+                d = lax.rem(t - b + nb, nb)
+
+                @pl.when(d != 0)
+                def _():
+                    copy(src, dst.at[b], ss.at[d], rs.at[b], b_dev(d)[1]).start()
+
+            return [copy(src, dst.at[b], ss.at[d], rs.at[b], b_dev(d)[1]) for d in order_b]
+
         barrier = pltpu.get_barrier_semaphore()
         for d in order_b:
             pl.semaphore_signal(barrier, inc=1, device_id=b_dev(d)[1], device_id_type=MESH)
@@ -197,10 +207,14 @@
         picked = dot_nt(pick, counts).astype(BF16)
         usable = dot_nn(picked, ex[...])
 
+        for h in range(heads):
+            us[h] = usable[h : h + 1]
         lanes = lax.broadcasted_iota(jnp.int32, (block_rows, 128), 1)
         stats = jnp.zeros((block_rows, 128), F32)
-        for h in range(heads):
-            s = jnp.where(usable[h : h + 1] > 0.5, s_ref[h], FLOOR)
+        own = lax.div(a, per_head)
+        for step in sorted(range(heads), key=lambda i: (i == 0, -min(i, heads - i))):
+            h = lax.rem(own + step, heads)
+            s = jnp.where(us[h] > 0.5, s_ref[h], FLOOR)
             top = jnp.max(s, axis=1, keepdims=True)
             offset = jnp.where(top > 0.5 * FLOOR, top, 0.0)
             p = jnp.exp(s - offset).astype(BF16)
@@ -212,19 +226,26 @@
                 part = slice(i * block_rows, (i + 1) * block_rows)
                 o1s[h * per_head + i] = o[part].astype(BF16)
                 stats = jnp.where(lanes == h * per_head + i, lse[part], stats)
+            for i in range(per_head):
+                if step == 0 and i == 0:
+                    continue
+                t = h * per_head + (lax.rem(a + i, per_head) if step == 0 else i)
+                k = step * per_head + i
+                r = copy(o1s.at[t], o1r.at[a], o1_send.at[k], o1_recv.at[a], a_dev(lax.rem(t - a + na, na))[1])
+                r.start()
+                sent.append(r)
         stats = flip(stats)
         for i in range(na):
             l1s[i] = stats[i : i + 1]
         l1r[a] = l1s[a]
         o1r[a] = o1s[a]
         sent += send(a_dev, order_a, lambda t: l1s.at[t], l1r, a, l1_send, l1_recv)
-        sent += send(a_dev, order_a, lambda t: o1s.at[t], o1r, a, o1_send, o1_recv)
         wait_all(a_dev, order_a, lambda t: l1s.at[t], l1r, na, l1_send, l1_recv)
         w, lse = merge_weights(rows_of(l1r, na))
         w = flip(w)[0:block_rows]
         l2s[...] = lse
         l2r[b] = lse
-        sent += send(b_dev, order_b, lambda t: l2s, l2r, b, l2_send, l2_recv)
+        sent += send_pairs(l2s, l2r, l2_send, l2_recv)
         wait_all(a_dev, order_a, lambda t: o1s.at[t], o1r, na, o1_send, o1_recv)
         o = w[:, 0:1] * o1r[0].astype(F32)
         for i in range(1, na):
@@ -232,7 +253,7 @@
         o = o.astype(BF16)
         o2s[...] = o
         o2r[b] = o
-        sent += send(b_dev, order_b, lambda t: o2s, o2r, b, o2_send, o2_recv)
+        sent += send_pairs(o2s, o2r, o2_send, o2_recv)
         wait_all(b_dev, order_b, lambda t: l2s, l2r, nb, l2_send, l2_recv)
         w, _ = merge_weights(jnp.concatenate([lf, rows_of(l2r, nb)], axis=0))
         w = flip(w)[0:block_rows]
@@ -280,6 +301,7 @@
         pltpu.VMEM((drafts, width), BF16),
         pltpu.VMEM((na, drafts, width), BF16),
         pltpu.VMEM((128, tokens), BF16),
+        pltpu.VMEM((heads, 1, tokens), F32),
         dma((heads,)), dma((heads,)),
         dma((nb,)), dma((nb,)), dma((na,)), dma((na,)),
         dma((na,)), dma((na,)), dma((na,)), dma((na,)),
@@ -294,7 +316,7 @@
         out_specs=vmem,
         scratch_shapes=scratch,
         compiler_params=pltpu.CompilerParams(
-            collective_id=0, has_side_effects=True, vmem_limit_bytes=60 * 1024 * 1024
+            collective_id=0, has_side_effects=True, vmem_limit_bytes=52000 * 1024
         ),
     )
 

time: 60.1 us -> 62.1 us (1.033)
  local copies, waits for them, and re-layouts: 1.57 us -> 3.75 us
    unnamed x1 -> x9, local copies, waits for them, and re-layouts: 1.57 us -> 3.75 us
where the time goes in v3:
time: 62.1 us; the launch traced here: 61.8 us
  Pallas kernels  58.1 us (94%)
  local copies, waits for them, and re-layouts  3.75 us (6%)
    pallas_call x1, Pallas kernels, on_device(): call(queries, chosen.T, new_keys, new_values, key_cache.reshape(-1, span)...  58.1 us
    unnamed x9, local copies, waits for them, and re-layouts  3.75 us

profile of v3, /device:TPU:33, one launch (start us, length us, event | category | flops | bytes accessed | tf_op | source)
XLA Modules:
  0.0 61.8 jit_solution(3146400288403647092)
XLA Ops:
  0.0 0.0 copy-start
  0.0 0.9 %copy-done = bf16[16,4096]{1,0:T(8,128)(2,1)S(1)} copy-done((bf16[16,4096]{1,0:T(8,128)(2,1)S(1)}, bf16[16,4096]{1,0:T(8,128)(2,1)}, u32[]{:S(2)}) %copy-start) | copy-done | bytes 131096
  0.9 0.0 copy-start.1
  0.9 0.8 %copy-done.1 = bf16[16,1024]{1,0:T(8,128)(2,1)S(1)} copy-done((bf16[16,1024]{1,0:T(8,128)(2,1)S(1)}, bf16[16,1024]{1,0:T(8,128)(2,1)}, u32[]{:S(2)}) %copy-start.1) | copy-done | bytes 32792
  1.7 0.0 copy-start.2
  1.7 0.8 %copy-done.2 = bf16[16,1024]{1,0:T(8,128)(2,1)S(1)} copy-done((bf16[16,1024]{1,0:T(8,128)(2,1)S(1)}, bf16[16,1024]{1,0:T(8,128)(2,1)}, u32[]{:S(2)}) %copy-start.2) | copy-done | bytes 32792
  2.4 0.0 copy-start.3
  2.4 0.7 %copy-done.3 = s32[8,2]{0,1:T(2,128)S(1)} copy-done((s32[8,2]{0,1:T(2,128)S(1)}, s32[8,2]{0,1:T(2,128)}, u32[]{:S(2)}) %copy-start.3) | copy-done | bytes 88
  3.1 58.1 %shard_map.64 = bf16[16,4096]{1,0:T(8,128)(2,1)S(1)} custom-call(bf16[16,4096]{1,0:T(8,128)(2,1)S(1)} %copy-done, s32[2,8]{1,0:T(2,128)S(1)} %bitcast.3, bf16[16,1024]{1,0:T(8,128)(2,1)S(1)} %copy-done.1, bf16[16,1024]{1,0:T(8,128)(2,1)S(1)} %copy-done.2, bf16[2048,1024]{1,0:T(8,128)(2,1)} %bitcast.4, bf16[2048,1024]{1,0:T(8,128)(2,1)} %bitcast.5), custom_call_target="tpu_custom_call" | custom-call | tf_op jit(solution)/shard_map/pallas_call | solution.py:339
  61.2 0.7 %copy.8 = bf16[16,4096]{1,0:T(8,128)(2,1)} copy(bf16[16,4096]{1,0:T(8,128)(2,1)S(1)} %shard_map.64) | data formatting | bytes 262144
Async XLA Ops:
  0.0 0.9 %copy-start = (bf16[16,4096]{1,0:T(8,128)(2,1)S(1)}, bf16[16,4096]{1,0:T(8,128)(2,1)}, u32[]{:S(2)}) copy-start(bf16[16,4096]{1,0:T(8,128)(2,1)} %q_hbm.1) | copy-start | bytes 393220
  0.9 0.8 %copy-start.1 = (bf16[16,1024]{1,0:T(8,128)(2,1)S(1)}, bf16[16,1024]{1,0:T(8,128)(2,1)}, u32[]{:S(2)}) copy-start(bf16[16,1024]{1,0:T(8,128)(2,1)} %nk_hbm.1) | copy-start | bytes 98308
  1.7 0.8 %copy-start.2 = (bf16[16,1024]{1,0:T(8,128)(2,1)S(1)}, bf16[16,1024]{1,0:T(8,128)(2,1)}, u32[]{:S(2)}) copy-start(bf16[16,1024]{1,0:T(8,128)(2,1)} %nv_hbm.1) | copy-start | bytes 98308
  2.4 0.7 %copy-start.3 = (s32[8,2]{0,1:T(2,128)S(1)}, s32[8,2]{0,1:T(2,128)}, u32[]{:S(2)}) copy-start(s32[8,2]{0,1:T(2,128)} %param.11) | copy-start | bytes 196

commit v4 on v2

--- a/solution.py
+++ b/solution.py
@@ -93,18 +93,13 @@
             )
 
         def send(group, order, src, dst, me, ss, rs):
-            started = []
             for d in order:
                 t, dev = group(d)
-                r = copy(src(t), dst.at[me], ss.at[d], rs.at[me], dev)
-                r.start()
-                started.append(r)
-            return started
-
-        def wait_all(group, order, src, dst, n, ss, rs):
-            for d in order[::-1]:
-                t, dev = group(n - d)
-                copy(src(t), dst.at[t], ss.at[n - d], rs.at[t], dev).wait_recv()
+                copy(src(t), dst.at[me], ss, rs, dev).start()
+
+        def wait_bytes(buf, count, sem):
+            part = buf.at[pl.ds(0, count)]
+            pltpu.make_async_copy(part, part, sem).wait()
 
         small = [
             pltpu.make_async_copy(src, dst, small_sem.at[i])
@@ -113,6 +108,14 @@
             )
         ]
         small[0].start()
+        def send_pairs(src, dst, ss, rs):
+            for t in range(nb):
+                d = lax.rem(t - b + nb, nb)
+
+                @pl.when(d != 0)
+                def _():
+                    copy(src, dst.at[b], ss, rs, b_dev(d)[1]).start()
+
         barrier = pltpu.get_barrier_semaphore()
         for d in order_b:
             pl.semaphore_signal(barrier, inc=1, device_id=b_dev(d)[1], device_id_type=MESH)
@@ -120,7 +123,7 @@
             pl.semaphore_signal(barrier, inc=1, device_id=a_dev(d)[1], device_id_type=MESH)
 
         def load(src, dst, sem, h):
-            return pltpu.make_async_copy(src.at[:, pl.ds(h * 128, 128)], dst.at[h], sem.at[h])
+            return pltpu.make_async_copy(src.at[:, pl.ds(h * 128, 128)], dst.at[h], sem)
 
         for r in small[1:]:
             r.start()
@@ -138,7 +141,6 @@
         idbr[b] = idbs[...]
 
         def scores(h):
-            load(k_hbm, ks, k_sem, h).wait()
             base = h * groups * 128
             q = jnp.concatenate(
                 [q_ref[:, base + g * 128 : base + (g + 1) * 128] for g in range(groups)], axis=0
@@ -146,9 +148,10 @@
             s_ref[h] = dot_nt(q, ks[h]) * scaling
 
         pl.semaphore_wait(barrier, na - 1 + nb - 1)
-        sent = send(b_dev, order_b, lambda t: idbs, idbr, b, b_send, b_recv)
+        send(b_dev, order_b, lambda t: idbs, idbr, b, b_send, b_recv)
         for r in small[1:]:
             r.wait()
+        wait_bytes(ks, heads, k_sem)
         for h in range(heads):
             scores(h)
 
@@ -175,16 +178,15 @@
         row_page = lax.broadcasted_iota(jnp.int32, (128, tokens), 0)
         ex[...] = (key_page == row_page).astype(F32).astype(BF16)
 
-        wait_all(b_dev, order_b, lambda t: idbs, idbr, nb, b_send, b_recv)
+        wait_bytes(idbr, nb - 1, b_recv)
         joined = idbr[0]
         for i in range(1, nb):
             joined = joined + idbr[i]
         idas[...] = joined
         idar[a] = joined
-        sent += send(a_dev, order_a, lambda t: idas, idar, a, a_send, a_recv)
-        for h in range(heads):
-            load(v_hbm, vs, v_sem, h).wait()
-        wait_all(a_dev, order_a, lambda t: idas, idar, na, a_send, a_recv)
+        send(a_dev, order_a, lambda t: idas, idar, a, a_send, a_recv)
+        wait_bytes(vs, heads, v_sem)
+        wait_bytes(idar, na - 1, a_recv)
 
         local = rows_of(idar, na) - ((z * nx + x) * nc + c) * pages
         counts = [
@@ -212,32 +214,32 @@
                 part = slice(i * block_rows, (i + 1) * block_rows)
                 o1s[h * per_head + i] = o[part].astype(BF16)
                 stats = jnp.where(lanes == h * per_head + i, lse[part], stats)
+        send(a_dev, order_a, lambda t: o1s.at[t], o1r, a, o1_send, o1_recv)
+        o1r[a] = o1s[a]
         stats = flip(stats)
         for i in range(na):
             l1s[i] = stats[i : i + 1]
         l1r[a] = l1s[a]
-        o1r[a] = o1s[a]
-        sent += send(a_dev, order_a, lambda t: l1s.at[t], l1r, a, l1_send, l1_recv)
-        sent += send(a_dev, order_a, lambda t: o1s.at[t], o1r, a, o1_send, o1_recv)
-        wait_all(a_dev, order_a, lambda t: l1s.at[t], l1r, na, l1_send, l1_recv)
+        send(a_dev, order_a, lambda t: l1s.at[t], l1r, a, l1_send, l1_recv)
+        wait_bytes(l1r, na - 1, l1_recv)
         w, lse = merge_weights(rows_of(l1r, na))
         w = flip(w)[0:block_rows]
         l2s[...] = lse
         l2r[b] = lse
-        sent += send(b_dev, order_b, lambda t: l2s, l2r, b, l2_send, l2_recv)
-        wait_all(a_dev, order_a, lambda t: o1s.at[t], o1r, na, o1_send, o1_recv)
+        send_pairs(l2s, l2r, l2_send, l2_recv)
+        wait_bytes(o1r, na - 1, o1_recv)
         o = w[:, 0:1] * o1r[0].astype(F32)
         for i in range(1, na):
             o = o + w[:, i : i + 1] * o1r[i].astype(F32)
         o = o.astype(BF16)
         o2s[...] = o
         o2r[b] = o
-        sent += send(b_dev, order_b, lambda t: o2s, o2r, b, o2_send, o2_recv)
-        wait_all(b_dev, order_b, lambda t: l2s, l2r, nb, l2_send, l2_recv)
+        send_pairs(o2s, o2r, o2_send, o2_recv)
+        wait_bytes(l2r, nb - 1, l2_recv)
         w, _ = merge_weights(jnp.concatenate([lf, rows_of(l2r, nb)], axis=0))
         w = flip(w)[0:block_rows]
         o = w[:, 0:1] * of
-        wait_all(b_dev, order_b, lambda t: o2s, o2r, nb, o2_send, o2_recv)
+        wait_bytes(o2r, nb - 1, o2_recv)
         for i in range(nb):
             o = o + w[:, i + 1 : i + 2] * o2r[i].astype(F32)
         o = o.astype(BF16)
@@ -246,12 +248,17 @@
         )
         fs[...] = block
         fr[a] = block
-        sent += send(a_dev, order_a, lambda t: fs, fr, a, f_send, f_recv)
-        wait_all(a_dev, order_a, lambda t: fs, fr, na, f_send, f_recv)
+        send(a_dev, order_a, lambda t: fs, fr, a, f_send, f_recv)
+        wait_bytes(fr, na - 1, f_recv)
         for i in range(na):
             out_ref[:, i * width : (i + 1) * width] = fr[i]
-        for r in sent:
-            r.wait_send()
+        wait_bytes(idbr, nb - 1, b_send)
+        wait_bytes(idar, na - 1, a_send)
+        wait_bytes(o1r, na - 1, o1_send)
+        wait_bytes(l1r, na - 1, l1_send)
+        wait_bytes(o2r, nb - 1, o2_send)
+        wait_bytes(l2r, nb - 1, l2_send)
+        wait_bytes(fr, na - 1, f_send)
 
     dma = pltpu.SemaphoreType.DMA
     span = heads * 128
@@ -280,10 +287,7 @@
         pltpu.VMEM((drafts, width), BF16),
         pltpu.VMEM((na, drafts, width), BF16),
         pltpu.VMEM((128, tokens), BF16),
-        dma((heads,)), dma((heads,)),
-        dma((nb,)), dma((nb,)), dma((na,)), dma((na,)),
-        dma((na,)), dma((na,)), dma((na,)), dma((na,)),
-        dma((nb,)), dma((nb,)), dma((nb,)), dma((nb,)), dma((na,)), dma((na,)),
+        *[dma] * 16,
     ]
     vmem = pl.BlockSpec(memory_space=pltpu.VMEM)
     hbm = pl.BlockSpec(memory_space=pltpu.HBM)
@@ -294,7 +298,7 @@
         out_specs=vmem,
         scratch_shapes=scratch,
         compiler_params=pltpu.CompilerParams(
-            collective_id=0, has_side_effects=True, vmem_limit_bytes=60 * 1024 * 1024
+            collective_id=0, has_side_effects=True, vmem_limit_bytes=32 * 1024 * 1024
         ),
     )
 
@@ -315,8 +319,13 @@
             (span // heads) ** (-0.5),
         )
         return call(
-            queries, chosen.T, new_keys, new_values,
-            key_cache.reshape(-1, span), value_cache.reshape(-1, span),
+            *[
+                pltpu.with_memory_space_constraint(x, pltpu.HBM)
+                for x in (
+                    queries, chosen.T, new_keys, new_values,
+                    key_cache.reshape(-1, span), value_cache.reshape(-1, span),
+                )
+            ]
         )
 
     in_specs = (

time: 60.1 us -> 56.3 us (0.937)
  Pallas kernels: 58.4 us -> 55.6 us
  local copies, waits for them, and re-layouts: 1.57 us -> 0.66 us
    pallas_call x1, Pallas kernels: 58.4 us -> 55.6 us  [on_device(): call(*[pltpu.with_memory_space_constraint(x, pltpu.HBM) for x in (queries...]
    unnamed x1, local copies, waits for them, and re-layouts: 1.57 us -> 0.66 us
where the time goes in v4:
time: 56.3 us; the launch traced here: 56.2 us
  Pallas kernels  55.6 us (99%)
  local copies, waits for them, and re-layouts  0.66 us (1%)
    pallas_call x1, Pallas kernels, on_device(): call(*[pltpu.with_memory_space_constraint(x, pltpu.HBM) for x in (queries...  55.6 us

profile of v4, /device:TPU:33, one launch (start us, length us, event | category | flops | bytes accessed | tf_op | source)
XLA Modules:
  0.0 56.2 jit_solution(17445756330925519148)
XLA Ops:
  0.0 55.6 %shard_map.64 = bf16[16,4096]{1,0:T(8,128)(2,1)S(1)} custom-call(bf16[16,4096]{1,0:T(8,128)(2,1)} %q_hbm.1, s32[2,8]{1,0:T(2,128)} %bitcast.5, bf16[16,1024]{1,0:T(8,128)(2,1)} %nk_hbm.1, bf16[16,1024]{1,0:T(8,128)(2,1)} %nv_hbm.1, bf16[2048,1024]{1,0:T(8,128)(2,1)} %bitcast.3, bf16[2048,1024]{1,0:T(8,128)(2,1)} %bitcast.4), custom_call_target="tpu_custom_call" | custom-call | tf_op jit(solution)/shard_map/pallas_call | solution.py:321
  55.6 0.7 %copy.8 = bf16[16,4096]{1,0:T(8,128)(2,1)} copy(bf16[16,4096]{1,0:T(8,128)(2,1)S(1)} %shard_map.64) | data formatting | bytes 262144

commit v5 on v4

--- a/solution.py
+++ b/solution.py
@@ -57,9 +57,9 @@
 
     def kernel(
         q_hbm, ids_hbm, nk_hbm, nv_hbm, k_hbm, v_hbm, out_ref,
-        q_ref, ids_ref, nk_ref, nv_ref, small_sem, ks, vs, s_ref, idbs, idbr, idas, idar,
+        q_ref, ids_ref, nk_ref, nv_ref, small_sem, ks, vs, s_ref, ups, upr, idbs, idbr, idas, idar,
         o1s, l1s, o1r, l1r, o2s, l2s, o2r, l2r, fs, fr, ex,
-        k_sem, v_sem, b_send, b_recv, a_send, a_recv,
+        k_sem, v_sem, up_send, up_recv, b_send, b_recv, a_send, a_recv,
         o1_send, o1_recv, l1_send, l1_recv,
         o2_send, o2_recv, l2_send, l2_recv, f_send, f_recv,
     ):
@@ -83,6 +83,9 @@
             t = lax.rem(b + d, nb)
             return t, {"page_0": t * 2 + zlow, "page_1": x, "page_2": c}
 
+        def pair_dev(t):
+            return {"page_0": t * 2 + zlow, "page_1": x, "page_2": c}
+
         order_a = far_first(na, nc * 2)
         order_b = far_first(nb, 1)
 
@@ -108,6 +111,7 @@
             )
         ]
         small[0].start()
+
         def send_pairs(src, dst, ss, rs):
             for t in range(nb):
                 d = lax.rem(t - b + nb, nb)
@@ -117,10 +121,13 @@
                     copy(src, dst.at[b], ss, rs, b_dev(d)[1]).start()
 
         barrier = pltpu.get_barrier_semaphore()
-        for d in order_b:
-            pl.semaphore_signal(barrier, inc=1, device_id=b_dev(d)[1], device_id_type=MESH)
         for d in order_a:
             pl.semaphore_signal(barrier, inc=1, device_id=a_dev(d)[1], device_id_type=MESH)
+        for t in range(nb):
+
+            @pl.when((t == b - 1) | (t > b))
+            def _():
+                pl.semaphore_signal(barrier, inc=1, device_id=pair_dev(t), device_id_type=MESH)
 
         def load(src, dst, sem, h):
             return pltpu.make_async_copy(src.at[:, pl.ds(h * 128, 128)], dst.at[h], sem)
@@ -138,7 +145,16 @@
         ids = ids_ref[...]
         ids = jnp.concatenate([ids[j : j + 1] for j in range(ids.shape[0])] * nb, axis=1)
         idbs[...] = jnp.where(lax.div(lane, slot) == b, ids, 0)
-        idbr[b] = idbs[...]
+        for t in range(nb):
+
+            @pl.when(t <= b)
+            def _():
+                idbr[t] = jnp.zeros((1, 128), jnp.int32)
+
+        @pl.when(b == 0)
+        def _():
+            upr[...] = jnp.zeros((1, 128), jnp.int32)
+
 
         def scores(h):
             base = h * groups * 128
@@ -147,14 +163,47 @@
             )
             s_ref[h] = dot_nt(q, ks[h]) * scaling
 
-        pl.semaphore_wait(barrier, na - 1 + nb - 1)
-        send(b_dev, order_b, lambda t: idbs, idbr, b, b_send, b_recv)
-        for r in small[1:]:
+        def all_scores():
+            small[1].wait()
+            wait_bytes(ks, heads, k_sem)
+            for h in range(heads):
+                scores(h)
+
+        def up():
+            return copy(ups, upr, up_send, up_recv, pair_dev(lax.rem(b + 1, nb)))
+
+        def down(t):
+            return copy(idbs, idbr.at[b], b_send.at[t], b_recv.at[b], pair_dev(t))
+
+        early = b < nb - 3
+
+        @pl.when(early)
+        def _():
+            all_scores()
+
+        pl.semaphore_wait(barrier, na - 1 + b + (b < nb - 1).astype(jnp.int32))
+        for t in range(nb):
+
+            @pl.when(t < b)
+            def _():
+                down(t).start()
+
+        @pl.when(jnp.logical_not(early))
+        def _():
+            all_scores()
+
+        @pl.when(b > 0)
+        def _():
+            up().wait_recv()
+
+        ups[...] = upr[...] + idbs[...]
+
+        @pl.when(b < nb - 1)
+        def _():
+            up().start()
+
+        for r in small[2:]:
             r.wait()
-        wait_bytes(ks, heads, k_sem)
-        for h in range(heads):
-            scores(h)
-
         cols = pl.multiple_of(a * width, width)
         head_cols = pl.multiple_of(lax.div(a, per_head) * 128, 128)
         q_own = q_ref[:, pl.ds(cols, width)]
@@ -178,9 +227,14 @@
         row_page = lax.broadcasted_iota(jnp.int32, (128, tokens), 0)
         ex[...] = (key_page == row_page).astype(F32).astype(BF16)
 
-        wait_bytes(idbr, nb - 1, b_recv)
-        joined = idbr[0]
-        for i in range(1, nb):
+        for t in range(nb):
+
+            @pl.when(t > b)
+            def _():
+                copy(idbs, idbr.at[t], b_send.at[t], b_recv.at[t], pair_dev(t)).wait_recv()
+
+        joined = ups[...]
+        for i in range(nb):
             joined = joined + idbr[i]
         idas[...] = joined
         idar[a] = joined
@@ -214,13 +268,13 @@
                 part = slice(i * block_rows, (i + 1) * block_rows)
                 o1s[h * per_head + i] = o[part].astype(BF16)
                 stats = jnp.where(lanes == h * per_head + i, lse[part], stats)
-        send(a_dev, order_a, lambda t: o1s.at[t], o1r, a, o1_send, o1_recv)
-        o1r[a] = o1s[a]
         stats = flip(stats)
         for i in range(na):
             l1s[i] = stats[i : i + 1]
         l1r[a] = l1s[a]
         send(a_dev, order_a, lambda t: l1s.at[t], l1r, a, l1_send, l1_recv)
+        send(a_dev, order_a, lambda t: o1s.at[t], o1r, a, o1_send, o1_recv)
+        o1r[a] = o1s[a]
         wait_bytes(l1r, na - 1, l1_recv)
         w, lse = merge_weights(rows_of(l1r, na))
         w = flip(w)[0:block_rows]
@@ -252,7 +306,16 @@
         wait_bytes(fr, na - 1, f_recv)
         for i in range(na):
             out_ref[:, i * width : (i + 1) * width] = fr[i]
-        wait_bytes(idbr, nb - 1, b_send)
+        for t in range(nb):
+
+            @pl.when(t < b)
+            def _():
+                down(t).wait_send()
+
+        @pl.when(b < nb - 1)
+        def _():
+            up().wait_send()
+
         wait_bytes(idar, na - 1, a_send)
         wait_bytes(o1r, na - 1, o1_send)
         wait_bytes(l1r, na - 1, l1_send)
@@ -272,6 +335,8 @@
         pltpu.VMEM((heads, tokens, 128), BF16),
         pltpu.VMEM((heads, tokens, 128), BF16),
         pltpu.VMEM((heads, rows, tokens), F32),
+        pltpu.VMEM((1, 128), jnp.int32),
+        pltpu.VMEM((1, 128), jnp.int32),
         pltpu.VMEM((1, 128), jnp.int32),
         pltpu.VMEM((nb, 1, 128), jnp.int32),
         pltpu.VMEM((1, 128), jnp.int32),
@@ -287,7 +352,7 @@
         pltpu.VMEM((drafts, width), BF16),
         pltpu.VMEM((na, drafts, width), BF16),
         pltpu.VMEM((128, tokens), BF16),
-        *[dma] * 16,
+        *[dma] * 4, dma((nb,)), dma((nb,)), *[dma] * 12,
     ]
     vmem = pl.BlockSpec(memory_space=pltpu.VMEM)
     hbm = pl.BlockSpec(memory_space=pltpu.HBM)

time: 56.3 us -> 68.4 us (1.21)
  Pallas kernels: 55.6 us -> 67.6 us
    pallas_call x1, Pallas kernels: 55.6 us -> 67.6 us  [on_device(): call(*[pltpu.with_memory_space_constraint(x, pltpu.HBM) for x in (queries...]
where the time goes in v5:
time: 68.4 us; the launch traced here: 68.3 us
  Pallas kernels  67.6 us (99%)
    pallas_call x1, Pallas kernels, on_device(): call(*[pltpu.with_memory_space_constraint(x, pltpu.HBM) for x in (queries...  67.6 us

profile of v5, /device:TPU:33, one launch (start us, length us, event | category | flops | bytes accessed | tf_op | source)
XLA Modules:
  0.0 68.3 jit_solution(16876997889788928801)
XLA Ops:
  0.0 67.6 %shard_map.64 = bf16[16,4096]{1,0:T(8,128)(2,1)S(1)} custom-call(bf16[16,4096]{1,0:T(8,128)(2,1)} %q_hbm.1, s32[2,8]{1,0:T(2,128)} %bitcast.5, bf16[16,1024]{1,0:T(8,128)(2,1)} %nk_hbm.1, bf16[16,1024]{1,0:T(8,128)(2,1)} %nv_hbm.1, bf16[2048,1024]{1,0:T(8,128)(2,1)} %bitcast.3, bf16[2048,1024]{1,0:T(8,128)(2,1)} %bitcast.4), custom_call_target="tpu_custom_call" | custom-call | tf_op jit(solution)/shard_map/pallas_call | solution.py:386
  67.6 0.7 copy.8

commit v6 on v4

--- a/solution.py
+++ b/solution.py
@@ -108,8 +108,9 @@
             )
         ]
         small[0].start()
-        def send_pairs(src, dst, ss, rs):
-            for t in range(nb):
+
+        def send_pairs(targets, src, dst, ss, rs):
+            for t in targets:
                 d = lax.rem(t - b + nb, nb)
 
                 @pl.when(d != 0)
@@ -214,19 +215,19 @@
                 part = slice(i * block_rows, (i + 1) * block_rows)
                 o1s[h * per_head + i] = o[part].astype(BF16)
                 stats = jnp.where(lanes == h * per_head + i, lse[part], stats)
-        send(a_dev, order_a, lambda t: o1s.at[t], o1r, a, o1_send, o1_recv)
-        o1r[a] = o1s[a]
         stats = flip(stats)
         for i in range(na):
             l1s[i] = stats[i : i + 1]
         l1r[a] = l1s[a]
         send(a_dev, order_a, lambda t: l1s.at[t], l1r, a, l1_send, l1_recv)
+        send(a_dev, order_a, lambda t: o1s.at[t], o1r, a, o1_send, o1_recv)
+        o1r[a] = o1s[a]
         wait_bytes(l1r, na - 1, l1_recv)
         w, lse = merge_weights(rows_of(l1r, na))
         w = flip(w)[0:block_rows]
         l2s[...] = lse
         l2r[b] = lse
-        send_pairs(l2s, l2r, l2_send, l2_recv)
+        send_pairs(range(nb), l2s, l2r, l2_send, l2_recv)
         wait_bytes(o1r, na - 1, o1_recv)
         o = w[:, 0:1] * o1r[0].astype(F32)
         for i in range(1, na):
@@ -234,8 +235,9 @@
         o = o.astype(BF16)
         o2s[...] = o
         o2r[b] = o
-        send_pairs(o2s, o2r, o2_send, o2_recv)
+        send_pairs(range(nb // 4), o2s, o2r, o2_send, o2_recv)
         wait_bytes(l2r, nb - 1, l2_recv)
+        send_pairs(range(nb // 4, nb), o2s, o2r, o2_send, o2_recv)
         w, _ = merge_weights(jnp.concatenate([lf, rows_of(l2r, nb)], axis=0))
         w = flip(w)[0:block_rows]
         o = w[:, 0:1] * of

time: 56.3 us -> 56.6 us (level)
  no operation moved by 1% of the time
where the time goes in v6:
time: 56.6 us; the launch traced here: 56.5 us
  Pallas kernels  55.8 us (99%)
  local copies, waits for them, and re-layouts  0.66 us (1%)
    pallas_call x1, Pallas kernels, on_device(): call(*[pltpu.with_memory_space_constraint(x, pltpu.HBM) for x in (queries...  55.8 us

profile of v6, /device:TPU:33, one launch (start us, length us, event | category | flops | bytes accessed | tf_op | source)
XLA Modules:
  0.0 56.5 jit_solution(4375407251975268515)
XLA Ops:
  0.0 55.8 %shard_map.64 = bf16[16,4096]{1,0:T(8,128)(2,1)S(1)} custom-call(bf16[16,4096]{1,0:T(8,128)(2,1)} %q_hbm.1, s32[2,8]{1,0:T(2,128)} %bitcast.5, bf16[16,1024]{1,0:T(8,128)(2,1)} %nk_hbm.1, bf16[16,1024]{1,0:T(8,128)(2,1)} %nv_hbm.1, bf16[2048,1024]{1,0:T(8,128)(2,1)} %bitcast.3, bf16[2048,1024]{1,0:T(8,128)(2,1)} %bitcast.4), custom_call_target="tpu_custom_call" | custom-call | tf_op jit(solution)/shard_map/pallas_call | solution.py:323
  55.8 0.7 %copy.8 = bf16[16,4096]{1,0:T(8,128)(2,1)} copy(bf16[16,4096]{1,0:T(8,128)(2,1)S(1)} %shard_map.64) | data formatting | bytes 262144

commit v7 on v4

--- a/solution.py
+++ b/solution.py
@@ -53,7 +53,8 @@
     pages = tokens // page_tokens
     block_rows = heads * groups * drafts // na
     per_head = na // heads
-    width = block_rows // drafts * 128
+    halves = block_rows // drafts
+    width = halves * 128
 
     def kernel(
         q_hbm, ids_hbm, nk_hbm, nv_hbm, k_hbm, v_hbm, out_ref,
@@ -108,6 +109,7 @@
             )
         ]
         small[0].start()
+
         def send_pairs(src, dst, ss, rs):
             for t in range(nb):
                 d = lax.rem(t - b + nb, nb)
@@ -214,13 +216,13 @@
                 part = slice(i * block_rows, (i + 1) * block_rows)
                 o1s[h * per_head + i] = o[part].astype(BF16)
                 stats = jnp.where(lanes == h * per_head + i, lse[part], stats)
-        send(a_dev, order_a, lambda t: o1s.at[t], o1r, a, o1_send, o1_recv)
-        o1r[a] = o1s[a]
         stats = flip(stats)
         for i in range(na):
             l1s[i] = stats[i : i + 1]
         l1r[a] = l1s[a]
         send(a_dev, order_a, lambda t: l1s.at[t], l1r, a, l1_send, l1_recv)
+        send(a_dev, order_a, lambda t: o1s.at[t], o1r, a, o1_send, o1_recv)
+        o1r[a] = o1s[a]
         wait_bytes(l1r, na - 1, l1_recv)
         w, lse = merge_weights(rows_of(l1r, na))
         w = flip(w)[0:block_rows]
@@ -228,37 +230,41 @@
         l2r[b] = lse
         send_pairs(l2s, l2r, l2_send, l2_recv)
         wait_bytes(o1r, na - 1, o1_recv)
-        o = w[:, 0:1] * o1r[0].astype(F32)
-        for i in range(1, na):
-            o = o + w[:, i : i + 1] * o1r[i].astype(F32)
-        o = o.astype(BF16)
-        o2s[...] = o
-        o2r[b] = o
-        send_pairs(o2s, o2r, o2_send, o2_recv)
+        for k in range(halves):
+            part = slice(k * drafts, (k + 1) * drafts)
+            o = w[part, 0:1] * o1r[0, part].astype(F32)
+            for i in range(1, na):
+                o = o + w[part, i : i + 1] * o1r[i, part].astype(F32)
+            o = o.astype(BF16)
+            o2s[k] = o
+            o2r[k, b] = o
+            send_pairs(o2s.at[k], o2r.at[k], o2_send.at[k], o2_recv.at[k])
         wait_bytes(l2r, nb - 1, l2_recv)
         w, _ = merge_weights(jnp.concatenate([lf, rows_of(l2r, nb)], axis=0))
         w = flip(w)[0:block_rows]
-        o = w[:, 0:1] * of
-        wait_bytes(o2r, nb - 1, o2_recv)
-        for i in range(nb):
-            o = o + w[:, i + 1 : i + 2] * o2r[i].astype(F32)
-        o = o.astype(BF16)
-        block = jnp.concatenate(
-            [o[i * drafts : (i + 1) * drafts] for i in range(width // 128)], axis=1
-        )
-        fs[...] = block
-        fr[a] = block
-        send(a_dev, order_a, lambda t: fs, fr, a, f_send, f_recv)
-        wait_bytes(fr, na - 1, f_recv)
-        for i in range(na):
-            out_ref[:, i * width : (i + 1) * width] = fr[i]
+        for k in range(halves):
+            part = slice(k * drafts, (k + 1) * drafts)
+            o = w[part, 0:1] * of[part]
+            wait_bytes(o2r.at[k], nb - 1, o2_recv.at[k])
+            for i in range(nb):
+                o = o + w[part, i + 1 : i + 2] * o2r[k, i].astype(F32)
+            o = o.astype(BF16)
+            fs[k] = o
+            fr[k, a] = o
+            send(a_dev, order_a, lambda t: fs.at[k], fr.at[k], a, f_send.at[k], f_recv.at[k])
+        for k in range(halves):
+            wait_bytes(fr.at[k], na - 1, f_recv.at[k])
+            for i in range(na):
+                at = i * width + k * 128
+                out_ref[:, at : at + 128] = fr[k, i]
         wait_bytes(idbr, nb - 1, b_send)
         wait_bytes(idar, na - 1, a_send)
         wait_bytes(o1r, na - 1, o1_send)
         wait_bytes(l1r, na - 1, l1_send)
-        wait_bytes(o2r, nb - 1, o2_send)
         wait_bytes(l2r, nb - 1, l2_send)
-        wait_bytes(fr, na - 1, f_send)
+        for k in range(halves):
+            wait_bytes(o2r.at[k], nb - 1, o2_send.at[k])
+            wait_bytes(fr.at[k], na - 1, f_send.at[k])
 
     dma = pltpu.SemaphoreType.DMA
     span = heads * 128
@@ -280,14 +286,14 @@
         pltpu.VMEM((na, 1, 128), F32),
         pltpu.VMEM((na, block_rows, 128), BF16),
         pltpu.VMEM((na, 1, 128), F32),
-        pltpu.VMEM((block_rows, 128), BF16),
+        pltpu.VMEM((halves, drafts, 128), BF16),
         pltpu.VMEM((1, 128), F32),
-        pltpu.VMEM((nb, block_rows, 128), BF16),
+        pltpu.VMEM((halves, nb, drafts, 128), BF16),
         pltpu.VMEM((nb, 1, 128), F32),
-        pltpu.VMEM((drafts, width), BF16),
-        pltpu.VMEM((na, drafts, width), BF16),
+        pltpu.VMEM((halves, drafts, 128), BF16),
+        pltpu.VMEM((halves, na, drafts, 128), BF16),
         pltpu.VMEM((128, tokens), BF16),
-        *[dma] * 16,
+        *[dma] * 10, *[dma((halves,))] * 2, *[dma] * 2, *[dma((halves,))] * 2,
     ]
     vmem = pl.BlockSpec(memory_space=pltpu.VMEM)
     hbm = pl.BlockSpec(memory_space=pltpu.HBM)

time: 56.3 us -> 56.4 us (level)
  no operation moved by 1% of the time
where the time goes in v7:
time: 56.4 us; the launch traced here: 56.3 us
  Pallas kernels  55.6 us (99%)
  local copies, waits for them, and re-layouts  0.66 us (1%)
    pallas_call x1, Pallas kernels, on_device(): call(*[pltpu.with_memory_space_constraint(x, pltpu.HBM) for x in (queries...  55.6 us

profile of v7, /device:TPU:33, one launch (start us, length us, event | category | flops | bytes accessed | tf_op | source)
XLA Modules:
  0.0 56.3 jit_solution(8058955193973566414)
XLA Ops:
  0.0 55.6 %shard_map.64 = bf16[16,4096]{1,0:T(8,128)(2,1)S(1)} custom-call(bf16[16,4096]{1,0:T(8,128)(2,1)} %q_hbm.1, s32[2,8]{1,0:T(2,128)} %bitcast.5, bf16[16,1024]{1,0:T(8,128)(2,1)} %nk_hbm.1, bf16[16,1024]{1,0:T(8,128)(2,1)} %nv_hbm.1, bf16[2048,1024]{1,0:T(8,128)(2,1)} %bitcast.3, bf16[2048,1024]{1,0:T(8,128)(2,1)} %bitcast.4), custom_call_target="tpu_custom_call" | custom-call | tf_op jit(solution)/shard_map/pallas_call | solution.py:327
  55.6 0.7 %copy.8 = bf16[16,4096]{1,0:T(8,128)(2,1)} copy(bf16[16,4096]{1,0:T(8,128)(2,1)S(1)} %shard_map.64) | data formatting | bytes 262144

commit v8 on v4

--- a/solution.py
+++ b/solution.py
@@ -47,10 +47,11 @@
     return sorted(range(1, n), key=key)
 
 
-def make_kernel(nz, nx, nc, heads, tokens, page_tokens, drafts, groups, scaling):
+def make_kernel(nz, nx, nc, heads, ids_each, tokens, page_tokens, drafts, groups, scaling):
     na = nx * nc * 2
     nb = nz // 2
     pages = tokens // page_tokens
+    id_rows = nz * ids_each // 128
     block_rows = heads * groups * drafts // na
     per_head = na // heads
     width = block_rows // drafts * 128
@@ -83,6 +84,16 @@
             t = lax.rem(b + d, nb)
             return t, {"page_0": t * 2 + zlow, "page_1": x, "page_2": c}
 
+        def z_dev(d):
+            t = lax.rem(z + d, nz)
+            return t, {"page_0": t, "page_1": x, "page_2": c}
+
+        def plane_dev(d):
+            t = lax.rem(x * nc + c + d, nx * nc)
+            return t, {"page_0": z, "page_1": lax.div(t, nc), "page_2": lax.rem(t, nc)}
+
+        order_z = far_first(nz, 1)
+        order_plane = far_first(nx * nc, nc)
         order_a = far_first(na, nc * 2)
         order_b = far_first(nb, 1)
 
@@ -108,6 +119,7 @@
             )
         ]
         small[0].start()
+
         def send_pairs(src, dst, ss, rs):
             for t in range(nb):
                 d = lax.rem(t - b + nb, nb)
@@ -117,8 +129,8 @@
                     copy(src, dst.at[b], ss, rs, b_dev(d)[1]).start()
 
         barrier = pltpu.get_barrier_semaphore()
-        for d in order_b:
-            pl.semaphore_signal(barrier, inc=1, device_id=b_dev(d)[1], device_id_type=MESH)
+        for d in order_z:
+            pl.semaphore_signal(barrier, inc=1, device_id=z_dev(d)[1], device_id_type=MESH)
         for d in order_a:
             pl.semaphore_signal(barrier, inc=1, device_id=a_dev(d)[1], device_id_type=MESH)
 
@@ -133,12 +145,13 @@
             load(v_hbm, vs, v_sem, h).start()
 
         lane = lax.broadcasted_iota(jnp.int32, (1, 128), 1)
-        slot = 128 // nb
+        slots = nz // id_rows
+        slot = 128 // slots
         small[0].wait()
         ids = ids_ref[...]
-        ids = jnp.concatenate([ids[j : j + 1] for j in range(ids.shape[0])] * nb, axis=1)
-        idbs[...] = jnp.where(lax.div(lane, slot) == b, ids, 0)
-        idbr[b] = idbs[...]
+        ids = jnp.concatenate([ids[j : j + 1] for j in range(ids.shape[0])] * slots, axis=1)
+        idbs[...] = jnp.where(lax.div(lane, slot) == lax.rem(z, slots), ids, 0)
+        idbr[z] = idbs[...]
 
         def scores(h):
             base = h * groups * 128
@@ -147,8 +160,8 @@
             )
             s_ref[h] = dot_nt(q, ks[h]) * scaling
 
-        pl.semaphore_wait(barrier, na - 1 + nb - 1)
-        send(b_dev, order_b, lambda t: idbs, idbr, b, b_send, b_recv)
+        pl.semaphore_wait(barrier, na - 1 + nz - 1)
+        send(z_dev, order_z, lambda t: idbs, idbr, z, b_send, b_recv)
         for r in small[1:]:
             r.wait()
         wait_bytes(ks, heads, k_sem)
@@ -178,17 +191,21 @@
         row_page = lax.broadcasted_iota(jnp.int32, (128, tokens), 0)
         ex[...] = (key_page == row_page).astype(F32).astype(BF16)
 
-        wait_bytes(idbr, nb - 1, b_recv)
-        joined = idbr[0]
-        for i in range(1, nb):
-            joined = joined + idbr[i]
-        idas[...] = joined
-        idar[a] = joined
-        send(a_dev, order_a, lambda t: idas, idar, a, a_send, a_recv)
+        wait_bytes(idbr, nz - 1, b_recv)
+        for r in range(id_rows):
+            joined = idbr[r * slots]
+            for i in range(r * slots + 1, (r + 1) * slots):
+                joined = joined + idbr[i]
+            idas[r] = joined
+            idar[x * nc + c, r] = joined
+        send(plane_dev, order_plane, lambda t: idas, idar, x * nc + c, a_send, a_recv)
         wait_bytes(vs, heads, v_sem)
-        wait_bytes(idar, na - 1, a_recv)
-
-        local = rows_of(idar, na) - ((z * nx + x) * nc + c) * pages
+        wait_bytes(idar, nx * nc - 1, a_recv)
+
+        local = jnp.concatenate(
+            [idar[i, r] for i in range(nx * nc) for r in range(id_rows)], axis=0
+        )
+        local = local - ((z * nx + x) * nc + c) * pages
         counts = [
             jnp.sum((local == p).astype(F32), axis=0, keepdims=True) for p in range(pages)
         ]
@@ -214,13 +231,13 @@
                 part = slice(i * block_rows, (i + 1) * block_rows)
                 o1s[h * per_head + i] = o[part].astype(BF16)
                 stats = jnp.where(lanes == h * per_head + i, lse[part], stats)
-        send(a_dev, order_a, lambda t: o1s.at[t], o1r, a, o1_send, o1_recv)
-        o1r[a] = o1s[a]
         stats = flip(stats)
         for i in range(na):
             l1s[i] = stats[i : i + 1]
         l1r[a] = l1s[a]
         send(a_dev, order_a, lambda t: l1s.at[t], l1r, a, l1_send, l1_recv)
+        send(a_dev, order_a, lambda t: o1s.at[t], o1r, a, o1_send, o1_recv)
+        o1r[a] = o1s[a]
         wait_bytes(l1r, na - 1, l1_recv)
         w, lse = merge_weights(rows_of(l1r, na))
         w = flip(w)[0:block_rows]
@@ -252,8 +269,8 @@
         wait_bytes(fr, na - 1, f_recv)
         for i in range(na):
             out_ref[:, i * width : (i + 1) * width] = fr[i]
-        wait_bytes(idbr, nb - 1, b_send)
-        wait_bytes(idar, na - 1, a_send)
+        wait_bytes(idbr, nz - 1, b_send)
+        wait_bytes(idar, nx * nc - 1, a_send)
         wait_bytes(o1r, na - 1, o1_send)
         wait_bytes(l1r, na - 1, l1_send)
         wait_bytes(o2r, nb - 1, o2_send)
@@ -265,7 +282,7 @@
     rows = heads * groups * drafts // heads
     scratch = [
         pltpu.VMEM((drafts, heads * groups * 128), BF16),
-        pltpu.VMEM((128 // nb // heads, heads), jnp.int32),
+        pltpu.VMEM((ids_each // heads, heads), jnp.int32),
         pltpu.VMEM((drafts, span), BF16),
         pltpu.VMEM((drafts, span), BF16),
         dma((4,)),
@@ -273,9 +290,9 @@
         pltpu.VMEM((heads, tokens, 128), BF16),
         pltpu.VMEM((heads, rows, tokens), F32),
         pltpu.VMEM((1, 128), jnp.int32),
-        pltpu.VMEM((nb, 1, 128), jnp.int32),
-        pltpu.VMEM((1, 128), jnp.int32),
-        pltpu.VMEM((na, 1, 128), jnp.int32),
+        pltpu.VMEM((nz, 1, 128), jnp.int32),
+        pltpu.VMEM((id_rows, 1, 128), jnp.int32),
+        pltpu.VMEM((nx * nc, id_rows, 1, 128), jnp.int32),
         pltpu.VMEM((na, block_rows, 128), BF16),
         pltpu.VMEM((na, 1, 128), F32),
         pltpu.VMEM((na, block_rows, 128), BF16),
@@ -315,7 +332,7 @@
         drafts = queries.shape[0]
         groups = queries.shape[1] // span
         call = make_kernel(
-            nz, nx, nc, heads, pages * page_tokens, page_tokens, drafts, groups,
+            nz, nx, nc, heads, chosen.size, pages * page_tokens, page_tokens, drafts, groups,
             (span // heads) ** (-0.5),
         )
         return call(

time: 56.3 us -> 56.4 us (level)
  no operation moved by 1% of the time
where the time goes in v8:
time: 56.4 us; the launch traced here: 56.3 us
  Pallas kernels  55.6 us (99%)
  local copies, waits for them, and re-layouts  0.66 us (1%)
    pallas_call x1, Pallas kernels, on_device(): call(*[pltpu.with_memory_space_constraint(x, pltpu.HBM) for x in (queries...  55.6 us

profile of v8, /device:TPU:33, one launch (start us, length us, event | category | flops | bytes accessed | tf_op | source)
XLA Modules:
  0.0 56.3 jit_solution(5184030329827055227)
XLA Ops:
  0.0 55.6 %shard_map.64 = bf16[16,4096]{1,0:T(8,128)(2,1)S(1)} custom-call(bf16[16,4096]{1,0:T(8,128)(2,1)} %q_hbm.1, s32[2,8]{1,0:T(2,128)} %bitcast.5, bf16[16,1024]{1,0:T(8,128)(2,1)} %nk_hbm.1, bf16[16,1024]{1,0:T(8,128)(2,1)} %nv_hbm.1, bf16[2048,1024]{1,0:T(8,128)(2,1)} %bitcast.3, bf16[2048,1024]{1,0:T(8,128)(2,1)} %bitcast.4), custom_call_target="tpu_custom_call" | custom-call | tf_op jit(solution)/shard_map/pallas_call | solution.py:338
  55.6 0.7 %copy.8 = bf16[16,4096]{1,0:T(8,128)(2,1)} copy(bf16[16,4096]{1,0:T(8,128)(2,1)S(1)} %shard_map.64) | data formatting | bytes 262144

commit v9 on v8

--- a/solution.py
+++ b/solution.py
@@ -80,9 +80,8 @@
                 "page_2": lax.rem(u, nc),
             }
 
-        def b_dev(d):
-            t = lax.rem(b + d, nb)
-            return t, {"page_0": t * 2 + zlow, "page_1": x, "page_2": c}
+        def pair_dev(t):
+            return {"page_0": t * 2 + zlow, "page_1": x, "page_2": c}
 
         def z_dev(d):
             t = lax.rem(z + d, nz)
@@ -95,7 +94,6 @@
         order_z = far_first(nz, 1)
         order_plane = far_first(nx * nc, nc)
         order_a = far_first(na, nc * 2)
-        order_b = far_first(nb, 1)
 
         def copy(src, dst, ss, rs, dev):
             return pltpu.make_async_remote_copy(
@@ -120,13 +118,24 @@
         ]
         small[0].start()
 
+        def after(i, own):
+            return i + (i >= own).astype(jnp.int32)
+
         def send_pairs(src, dst, ss, rs):
-            for t in range(nb):
-                d = lax.rem(t - b + nb, nb)
-
-                @pl.when(d != 0)
-                def _():
-                    copy(src, dst.at[b], ss, rs, b_dev(d)[1]).start()
+            for i in range(nb - 1):
+                copy(src, dst.at[b], ss, rs, pair_dev(after(i, b))).start()
+
+        def send_final(src, dst, ss, rs):
+            plane = nx * nc
+            for i in range(na - 1):
+                r = after(i, zlow * plane + x * nc + c)
+                u = lax.rem(r, plane)
+                dev = {
+                    "page_0": b * 2 + lax.div(r, plane),
+                    "page_1": lax.div(u, nc),
+                    "page_2": lax.rem(u, nc),
+                }
+                copy(src, dst.at[a], ss, rs, dev).start()
 
         barrier = pltpu.get_barrier_semaphore()
         for d in order_z:
@@ -265,7 +274,7 @@
         )
         fs[...] = block
         fr[a] = block
-        send(a_dev, order_a, lambda t: fs, fr, a, f_send, f_recv)
+        send_final(fs, fr, f_send, f_recv)
         wait_bytes(fr, na - 1, f_recv)
         for i in range(na):
             out_ref[:, i * width : (i + 1) * width] = fr[i]

time: 56.4 us -> 55.7 us (0.988)
  Pallas kernels: 55.6 us -> 54.9 us
    pallas_call x1, Pallas kernels: 55.6 us -> 54.9 us  [on_device(): call(*[pltpu.with_memory_space_constraint(x, pltpu.HBM) for x in (queries...]
where the time goes in v9:
time: 55.7 us; the launch traced here: 55.6 us
  Pallas kernels  54.9 us (99%)
  local copies, waits for them, and re-layouts  0.66 us (1%)
    pallas_call x1, Pallas kernels, on_device(): call(*[pltpu.with_memory_space_constraint(x, pltpu.HBM) for x in (queries...  54.9 us

profile of v9, /device:TPU:33, one launch (start us, length us, event | category | flops | bytes accessed | tf_op | source)
XLA Modules:
  0.0 55.6 jit_solution(57865457359079651)
XLA Ops:
  0.0 54.9 %shard_map.64 = bf16[16,4096]{1,0:T(8,128)(2,1)S(1)} custom-call(bf16[16,4096]{1,0:T(8,128)(2,1)} %q_hbm.1, s32[2,8]{1,0:T(2,128)} %bitcast.5, bf16[16,1024]{1,0:T(8,128)(2,1)} %nk_hbm.1, bf16[16,1024]{1,0:T(8,128)(2,1)} %nv_hbm.1, bf16[2048,1024]{1,0:T(8,128)(2,1)} %bitcast.3, bf16[2048,1024]{1,0:T(8,128)(2,1)} %bitcast.4), custom_call_target="tpu_custom_call" | custom-call | tf_op jit(solution)/shard_map/pallas_call | solution.py:347
  54.9 0.7 %copy.8 = bf16[16,4096]{1,0:T(8,128)(2,1)} copy(bf16[16,4096]{1,0:T(8,128)(2,1)S(1)} %shard_map.64) | data formatting | bytes 262144

commit v10 on v9

--- a/solution.py
+++ b/solution.py
@@ -146,12 +146,6 @@
         def load(src, dst, sem, h):
             return pltpu.make_async_copy(src.at[:, pl.ds(h * 128, 128)], dst.at[h], sem)
 
-        for r in small[1:]:
-            r.start()
-        for h in range(heads):
-            load(k_hbm, ks, k_sem, h).start()
-        for h in range(heads):
-            load(v_hbm, vs, v_sem, h).start()
 
         lane = lax.broadcasted_iota(jnp.int32, (1, 128), 1)
         slots = nz // id_rows
@@ -171,6 +165,12 @@
 
         pl.semaphore_wait(barrier, na - 1 + nz - 1)
         send(z_dev, order_z, lambda t: idbs, idbr, z, b_send, b_recv)
+        for r in small[1:]:
+            r.start()
+        for h in range(heads):
+            load(k_hbm, ks, k_sem, h).start()
+        for h in range(heads):
+            load(v_hbm, vs, v_sem, h).start()
         for r in small[1:]:
             r.wait()
         wait_bytes(ks, heads, k_sem)

time: 55.7 us -> 55.4 us (level)
  no operation moved by 1% of the time
where the time goes in v10:
time: 55.4 us; the launch traced here: 55.3 us
  Pallas kernels  54.6 us (99%)
  local copies, waits for them, and re-layouts  0.66 us (1%)
    pallas_call x1, Pallas kernels, on_device(): call(*[pltpu.with_memory_space_constraint(x, pltpu.HBM) for x in (queries...  54.6 us

profile of v10, /device:TPU:33, one launch (start us, length us, event | category | flops | bytes accessed | tf_op | source)
XLA Modules:
  0.0 55.3 jit_solution(17081320829288903852)
XLA Ops:
  0.0 54.6 %shard_map.64 = bf16[16,4096]{1,0:T(8,128)(2,1)S(1)} custom-call(bf16[16,4096]{1,0:T(8,128)(2,1)} %q_hbm.1, s32[2,8]{1,0:T(2,128)} %bitcast.5, bf16[16,1024]{1,0:T(8,128)(2,1)} %nk_hbm.1, bf16[16,1024]{1,0:T(8,128)(2,1)} %nv_hbm.1, bf16[2048,1024]{1,0:T(8,128)(2,1)} %bitcast.3, bf16[2048,1024]{1,0:T(8,128)(2,1)} %bitcast.4), custom_call_target="tpu_custom_call" | custom-call | tf_op jit(solution)/shard_map/pallas_call | solution.py:347
  54.6 0.7 %copy.8 = bf16[16,4096]{1,0:T(8,128)(2,1)} copy(bf16[16,4096]{1,0:T(8,128)(2,1)S(1)} %shard_map.64) | data formatting | bytes 262144
